TPU v7x, 512 devices: a whole 4x4x16 slice. The times are simulated.
512 devices in a mesh: head: 8 (over y, core), seq: 64 (over z, x).
Axes of the slice: x: 4, y: 4, z: 16, core: 2. Of those that a mesh axis runs over, the one named last changes fastest.
Arguments:
- queries: bfloat16 [64, 1024, 4096], P('seq', 'head'), may hold values from -6 to 6
- key_rows: bfloat16 [64, 1024, 4096], P('seq', 'head'), may hold values from -6 to 6
- value_rows: bfloat16 [64, 1024, 4096], P('seq', 'head'), may hold values from -6 to 6
- head_gain: float32 [4096], replicated, may hold values from 0.5 to 1.5
Outputs:
- attended: bfloat16 [64, 1024, 4096], P('seq', 'head')
All inputs are finite; a program needn't handle non-finite values.
Results may differ from a plain program's by a relative error of at most 0.0065.
Values may be sent and summed in bfloat16 or wider, within the bound.
No kernel may reach another device: no remote copies, remote signals or barrier semaphores. Data moves between devices by JAX's collectives and lax.ppermute only.
A program may use at most 64 MiB of HBM per device.

v0:
```python
import jax
import jax.numpy as jnp
from jax import lax
from jax.sharding import Mesh
from jax.sharding import PartitionSpec as P

DH = 128
BLOCK = 512
SEQ = ("seq_0", "seq_1")


epsilon = 1e-06


def nothing_yet(value, identity):
    return jnp.zeros_like(value) + jnp.asarray(identity, value.dtype)


def prefix_by_axis(value, axes, combine, identity):
    before = start = nothing_yet(value, identity)
    total = value
    for axis in reversed(axes):
        size, index = (lax.axis_size(axis), lax.axis_index(axis))
        pieces = lax.all_gather(total.astype(jnp.bfloat16), axis)
        inside, total = (start, start)
        for k in range(size):
            passed = k < index
            total = combine(total, pieces[k].astype(value.dtype))
            inside = jnp.where(passed, total, inside)
        before = combine(inside, before)
    return before


def activate(rows):
    return jax.nn.silu(rows.astype(jnp.float32)).astype(jnp.bfloat16)


def add_states(earlier, later):
    return earlier + later


def attend(pieces, chain):
    moved_q, moved_k, moved_v = pieces
    row_count = moved_q.shape[0]
    head_count = moved_q.shape[2]
    head_width = moved_q.shape[3]
    blocks = row_count // BLOCK
    block_q = moved_q.reshape(blocks, BLOCK, head_count, head_width)
    block_k = moved_k.reshape(blocks, BLOCK, head_count, head_width)
    block_v = moved_v.reshape(blocks, BLOCK, head_count, head_width)
    states = jnp.einsum("nbhd,nbhe->nhde", block_k, block_v, preferred_element_type=jnp.float32)
    span_total = jnp.sum(states, axis=0)
    incoming = chain(span_total)
    running = jnp.cumsum(states, axis=0)
    exclusive = jnp.concatenate([jnp.zeros_like(states[:1]), running[:-1]], axis=0)
    prefix = incoming[None] + exclusive
    scores = jnp.einsum("nihd,njhd->nhij", block_q, block_k, preferred_element_type=jnp.float32)
    row_pos = lax.broadcasted_iota(jnp.int32, (BLOCK, BLOCK), 0)
    col_pos = lax.broadcasted_iota(jnp.int32, (BLOCK, BLOCK), 1)
    scores = jnp.where(row_pos >= col_pos, scores, 0.0).astype(jnp.bfloat16)
    local_part = jnp.einsum("nhij,njhe->nihe", scores, block_v, preferred_element_type=jnp.float32)
    carried = jnp.einsum(
        "nihd,nhde->nihe", block_q.astype(jnp.float32), prefix, precision=lax.Precision.HIGHEST
    )
    results = (local_part + carried).reshape(row_count, 1, head_count, head_width)
    normed = results * lax.rsqrt(jnp.mean(results * results, axis=-1, keepdims=True) + epsilon)
    return normed.astype(jnp.bfloat16)


def local(queries, key_rows, value_rows, head_gain):
    local_rows = queries.shape[1]
    groups = lax.axis_size("head")
    head_width = DH
    per_group = queries.shape[2] // (groups * head_width)
    shape_four = (local_rows, groups, per_group, head_width)
    act_q = activate(queries[0]).reshape(shape_four)
    act_k = activate(key_rows[0]).reshape(shape_four)
    plain_v = value_rows[0].reshape(shape_four)

    def chain_whole(span_total):
        return prefix_by_axis(span_total, SEQ, add_states, jnp.zeros_like(span_total))

    moved = (
        lax.all_to_all(act_q, "head", split_axis=1, concat_axis=0, tiled=True),
        lax.all_to_all(act_k, "head", split_axis=1, concat_axis=0, tiled=True),
        lax.all_to_all(plain_v, "head", split_axis=1, concat_axis=0, tiled=True),
    )
    normed = attend(moved, chain_whole)
    restored = lax.all_to_all(normed, "head", split_axis=0, concat_axis=1, tiled=True)
    flat = restored.reshape(local_rows, groups * per_group * head_width)
    attended = (flat.astype(jnp.float32) * head_gain[None, :]).astype(jnp.bfloat16)
    return attended.reshape(1, local_rows, flat.shape[1])


def solution(mesh):
    torus = Mesh(mesh.devices.reshape(mesh.shape["head"], 16, 4), ("head", "seq_0", "seq_1"))
    in_specs = (P(SEQ, "head", None), P(SEQ, "head", None), P(SEQ, "head", None), P())
    out_specs = P(SEQ, "head", None)
    return jax.shard_map(local, mesh=torus, in_specs=in_specs, out_specs=out_specs, check_vma=False)
```

profile of v0, /device:TPU:1, one launch (start us, length us, event | category | flops | bytes accessed | tf_op | source)
XLA Modules:
  0.0 180.2 jit_solution(1239405842496762504)
XLA Ops:
  6.5 1.6 copy.33
  8.2 0.0 copy-start.2
  8.2 1.5 fusion.12
  9.7 10.3 %all-to-all-start.1 = ((bf16[128,8,4,128]{0,3,2,1:T(8,128)(2,1)}), bf16[128,8,4,128]{0,3,2,1:T(8,128)(2,1)S(1)}, u32[]{:S(2)}, u32[]{:S(2)}) async-start(bf16[128,8,4,128]{0,3,2,1:T(8,128)(2,1)} %fusion.12), calls=%async_computation.1 | async-start | bytes 2097152 | tf_op jit(solution)/shard_map/all_to_all | solution.py:85
  20.0 0.0 copy-done.2
  20.0 1.3 copy.37
  21.3 13.7 %all-to-all-done.1 = bf16[128,8,4,128]{0,3,2,1:T(8,128)(2,1)S(1)} async-done(((bf16[128,8,4,128]{0,3,2,1:T(8,128)(2,1)}), bf16[128,8,4,128]{0,3,2,1:T(8,128)(2,1)S(1)}, u32[]{:S(2)}, u32[]{:S(2)}) %all-to-all-start.1) | async-done | bytes 1048608 | tf_op jit(solution)/shard_map/all_to_all | solution.py:85
  35.0 4.4 %all-to-all-start.2 = ((bf16[128,8,4,128]{0,3,2,1:T(8,128)(2,1)}), bf16[128,8,4,128]{0,3,2,1:T(8,128)(2,1)S(1)}, u32[]{:S(2)}, u32[]{:S(2)}) async-start(bf16[128,8,4,128]{0,3,2,1:T(8,128)(2,1)} %bitcast.10), calls=%async_computation.2 | async-start | bytes 2097152 | tf_op jit(solution)/shard_map/all_to_all | solution.py:86
  39.4 0.0 all-gather.3.cloned.1.call-start
  39.4 1.3 copy.34
  40.7 0.0 copy-start.4
  40.7 13.7 %all-to-all-done.2 = bf16[128,8,4,128]{0,3,2,1:T(8,128)(2,1)S(1)} async-done(((bf16[128,8,4,128]{0,3,2,1:T(8,128)(2,1)}), bf16[128,8,4,128]{0,3,2,1:T(8,128)(2,1)S(1)}, u32[]{:S(2)}, u32[]{:S(2)}) %all-to-all-start.2) | async-done | bytes 1048608 | tf_op jit(solution)/shard_map/all_to_all | solution.py:86
  54.4 1.3 copy.38
  55.7 0.0 copy-done.4
  55.7 0.0 copy-start.3
  55.7 1.8 fusion.52
  57.5 9.9 %all-gather = bf16[16,128,128]{2,1,0:T(8,128)(2,1)S(1)} all-gather(bf16[4,128,128]{2,1,0:T(8,128)(2,1)S(1)} %get-tuple-element.5), channel_id=2, replica_groups=mesh['head'=8,'seq_0'=16,'seq_1'=4] {'seq_1'}, dimensions={0}, use_global_device_ids=true | all-gather | bytes 655360 | tf_op jit(solution)/shard_map/all_gather | solution.py:24
  67.4 0.7 fusion.49
  68.2 0.0 all-gather.3.cloned.1.call-update
  68.2 0.0 copy-done.3
  68.2 0.7 copy.31
  68.9 1.5 fusion.8
  70.4 7.7 %all-to-all-start = ((bf16[128,8,4,128]{0,3,2,1:T(8,128)(2,1)}), bf16[128,8,4,128]{0,3,2,1:T(8,128)(2,1)S(1)}, u32[]{:S(2)}, u32[]{:S(2)}) async-start(bf16[128,8,4,128]{0,3,2,1:T(8,128)(2,1)} %fusion.8), calls=%async_computation | async-start | bytes 2097152 | tf_op jit(solution)/shard_map/all_to_all | solution.py:84
  78.1 0.1 iota_compare_fusion
  78.2 14.9 %all-to-all-done = bf16[128,8,4,128]{0,3,2,1:T(8,128)(2,1)S(1)} async-done(((bf16[128,8,4,128]{0,3,2,1:T(8,128)(2,1)}), bf16[128,8,4,128]{0,3,2,1:T(8,128)(2,1)S(1)}, u32[]{:S(2)}, u32[]{:S(2)}) %all-to-all-start) | async-done | bytes 1048608 | tf_op jit(solution)/shard_map/all_to_all | solution.py:84
  93.1 0.7 copy.32
  93.8 0.2 fusion.53
  94.0 0.0 copy-start.1
  94.0 5.4 %fusion = f32[2,4,512,128]{3,2,1,0:T(8,128)} fusion(pred[512,512]{1,0:T(8,128)(4,1)S(1)} %iota_compare_fusion, bf16[2,512,4,128]{3,1,0,2:T(8,128)(2,1)} %bitcast.56, bf16[2,512,4,128]{3,1,0,2:T(8,128)(2,1)} %bitcast.53, bf16[2,512,4,128]{3,1,0,2:T(8,128)(2,1)S(1)} %bitcast.51), kind=kOutput, calls=%fused_computation.1 | convolution fusion | flops 1077936128 | bytes 5505024 | tf_op jit(solution)/shard_map/nhij,njhe->nihe/dot_general | solution.py:61
  99.5 0.0 copy-done.1
  99.5 34.4 %all-gather.3.cloned.1.call-done = bf16[16,4,128,128]{3,2,1,0:T(8,128)(2,1)} async-done(((bf16[1,4,128,128]{3,2,1,0:T(8,128)(2,1)}), bf16[16,4,128,128]{3,2,1,0:T(8,128)(2,1)}) %all-gather.3.cloned.1.call-update) | async-done | bytes 2097168 | tf_op jit(solution)/shard_map/all_gather | solution.py:24
  133.8 0.0 copy-start
  133.8 0.0 slice-start
  133.8 2.3 %fusion.48 = f32[4,128,128]{2,1,0:T(8,128)S(1)} fusion(bf16[16,4,128,128]{3,2,1,0:T(8,128)(2,1)} %all-gather.3.cloned.1.call-done, pred[]{:T(512)S(6)} %gt.76, pred[]{:T(512)S(6)} %gt.77, pred[]{:T(512)S(6)} %gt.78, pred[]{:T(512)S(6)} %gt.79, pred[]{:T(512)S(6)} %gt.75, pred[]{:T(512)S(6)} %gt.74, pred[]{:T(512)S(6)} %gt.73, pred[]{:T(512)S(6)} %gt.72, ...), kind=kLoop, calls=%fused_computation.62 | loop fusion | flops 3866624 | bytes 2883604 | tf_op jit(solution)/shard_map/add | solution.py:56
  136.1 0.0 copy-done
  136.1 0.0 slice-done
  136.1 1.6 multiply_reduce_fusion
  137.8 0.2 copy.45
  137.9 0.9 fusion.14
  138.8 0.8 copy.46
  139.6 28.3 %all_to_all.54 = bf16[1024,1,4,128]{3,2,1,0:T(4,128)(2,1)S(1)} all-to-all(bf16[1024,1,4,128]{3,2,1,0:T(4,128)(2,1)S(1)} %copy.46), channel_id=1, replica_groups=mesh['head'=8,'seq_0'=16,'seq_1'=4] {'head'}, dimensions={0} | all-to-all | bytes 2097152 | tf_op jit(solution)/shard_map/all_to_all | solution.py:89
  167.9 0.1 copy.47
  168.0 0.2 convert_bitcast_fusion
  168.3 0.0 copy-start.5
  168.3 1.9 %copy.48 = f32[128,8,1,4,128]{0,4,3,1,2:T(8,128)} copy(f32[128,8,1,4,128]{4,0,1,3,2:T(8,128)S(1)} %convert_bitcast_fusion) | data formatting | bytes 4194304 | tf_op jit(solution)/shard_map/convert_element_type | solution.py:91
  170.2 0.0 copy-done.5
  170.2 1.9 %fusion.13 = bf16[1,128,4096]{1,2,0:T(8,128)(2,1)S(1)} fusion(f32[128,8,1,4,128]{0,4,3,1,2:T(8,128)} %copy.48, f32[4096]{0:T(1024)S(1)} %copy-done.5), kind=kLoop, calls=%fused_computation.19 | loop fusion | flops 1048576 | bytes 3162112 | tf_op jit(solution)/shard_map/convert_element_type | solution.py:91
  172.1 1.3 copy.49
  (1 shorter events, 0.0 us)
Async XLA Ops:
  8.2 11.8 %copy-start.2 = (bf16[1,128,4096]{2,1,0:T(8,128)(2,1)S(1)}, bf16[1,128,4096]{2,1,0:T(8,128)(2,1)}, u32[]{:S(2)}) copy-start(bf16[1,128,4096]{2,1,0:T(8,128)(2,1)} %param.6) | copy-start | bytes 3145732
  9.7 25.3 %all-to-all-start.1 = ((bf16[128,8,4,128]{0,3,2,1:T(8,128)(2,1)}), bf16[128,8,4,128]{0,3,2,1:T(8,128)(2,1)S(1)}, u32[]{:S(2)}, u32[]{:S(2)}) async-start(bf16[128,8,4,128]{0,3,2,1:T(8,128)(2,1)} %fusion.12), calls=%async_computation.1 | async-start | bytes 2097152 | tf_op jit(solution)/shard_map/all_to_all | solution.py:85
  35.0 19.4 %all-to-all-start.2 = ((bf16[128,8,4,128]{0,3,2,1:T(8,128)(2,1)}), bf16[128,8,4,128]{0,3,2,1:T(8,128)(2,1)S(1)}, u32[]{:S(2)}, u32[]{:S(2)}) async-start(bf16[128,8,4,128]{0,3,2,1:T(8,128)(2,1)} %bitcast.10), calls=%async_computation.2 | async-start | bytes 2097152 | tf_op jit(solution)/shard_map/all_to_all | solution.py:86
  39.4 94.4 %all-gather.3.cloned.1.call-start = ((), (), s32[]{:S(2)}) async-start(), calls=%async_computation.4 | async-start | bytes 2228224 | tf_op jit(solution)/shard_map/all_gather | solution.py:24
  40.7 15.0 %copy-start.4 = (bf16[8,128,1,4,128]{4,1,0,3,2:T(8,128)(2,1)S(1)}, bf16[8,128,1,4,128]{4,1,0,3,2:T(8,128)(2,1)}, u32[]{:S(2)}) copy-start(bf16[8,128,1,4,128]{4,1,0,3,2:T(8,128)(2,1)} %copy.34) | copy-start | bytes 3145732
  55.7 12.5 %copy-start.3 = (bf16[1,128,4096]{2,1,0:T(8,128)(2,1)S(1)}, bf16[1,128,4096]{2,1,0:T(8,128)(2,1)}, u32[]{:S(2)}) copy-start(bf16[1,128,4096]{2,1,0:T(8,128)(2,1)} %param.4) | copy-start | bytes 3145732
  70.4 22.7 %all-to-all-start = ((bf16[128,8,4,128]{0,3,2,1:T(8,128)(2,1)}), bf16[128,8,4,128]{0,3,2,1:T(8,128)(2,1)S(1)}, u32[]{:S(2)}, u32[]{:S(2)}) async-start(bf16[128,8,4,128]{0,3,2,1:T(8,128)(2,1)} %fusion.8), calls=%async_computation | async-start | bytes 2097152 | tf_op jit(solution)/shard_map/all_to_all | solution.py:84
  94.0 5.4 %copy-start.1 = (f32[2,4,128,128]{3,2,1,0:T(8,128)}, f32[2,4,128,128]{3,2,1,0:T(8,128)S(1)}, u32[]{:S(2)}) copy-start(f32[2,4,128,128]{3,2,1,0:T(8,128)S(1)} %fusion.53) | copy-start | bytes 1572868
  133.8 2.3 %copy-start = (f32[2,4,512,128]{3,2,1,0:T(8,128)S(1)}, f32[2,4,512,128]{3,2,1,0:T(8,128)}, u32[]{:S(2)}) copy-start(f32[2,4,512,128]{3,2,1,0:T(8,128)} %fusion) | copy-start | bytes 6291460
  133.8 2.3 %slice-start = ((f32[2,4,128,128]{3,2,1,0:T(8,128)}), f32[1,4,128,128]{3,2,1,0:T(8,128)S(1)}, s32[]{:S(2)}) async-start(f32[2,4,128,128]{3,2,1,0:T(8,128)} %copy-done.1), calls=%async_computation.5 | async-start | bytes 524288 | tf_op jit(solution)/shard_map/slice | solution.py:55
  168.3 1.9 %copy-start.5 = (f32[4096]{0:T(1024)S(1)}, f32[4096]{0:T(1024)}, u32[]{:S(2)}) copy-start(f32[4096]{0:T(1024)} %param.7) | copy-start | bytes 49156
Sparse Core Ops, SparseCore 0:
  68.3 65.4 all-gather.2
where the time goes:
time: 181 us; the launch traced here: 180 us
  waiting for transfers between devices  76.7 us (42%)
  blocking collectives  38.2 us (21%)
  starting transfers between devices  22.5 us (12%)
  between operations  13.5 us (7%)
  local copies, waits for them, and re-layouts  11.2 us (6%)
  other arithmetic  9.42 us (5%)
  matrix products  8.83 us (5%)
    all_gather x1, waiting for transfers between devices, prefix_by_axis(): pieces = lax.all_gather(total.astype(jnp.bfloat16), axis)  34.4 us
    all_to_all x1, blocking collectives, local(): lax.all_to_all(normed, 'head', split_axis=0, concat_axis=1, tiled=True)  28.3 us
    all_to_all x1, waiting for transfers between devices, local(): lax.all_to_all(act_q, 'head', split_axis=1, concat_axis=0, tiled=True)  14.9 us
    all_to_all x1, waiting for transfers between devices, local(): lax.all_to_all(act_k, 'head', split_axis=1, concat_axis=0, tiled=True)  13.7 us
    all_to_all x1, waiting for transfers between devices, local(): lax.all_to_all(plain_v, 'head', split_axis=1, concat_axis=0, tiled=True)  13.7 us
    all_to_all x1, starting transfers between devices, local(): lax.all_to_all(act_k, 'head', split_axis=1, concat_axis=0, tiled=True)  10.3 us
    all_gather x1, blocking collectives, prefix_by_axis(): pieces = lax.all_gather(total.astype(jnp.bfloat16), axis)  9.9 us
    all_to_all x1, starting transfers between devices, local(): lax.all_to_all(act_q, 'head', split_axis=1, concat_axis=0, tiled=True)  7.73 us
  transfers between devices with their start and end apart: 4, of which 4 were waited for; matrix products, arithmetic and copies ran while one was open for 6% of the time, Pallas kernels for 0%

commit v1 on v0

v1 whole, which is shorter than its diff:
```python
import jax
import jax.numpy as jnp
from jax import lax
from jax.experimental import pallas as pl
from jax.experimental.pallas import tpu as pltpu
from jax.sharding import Mesh
from jax.sharding import PartitionSpec as P

DH = 128
EPSILON = 1e-06
PLANE = ("x", "y", "core")
bf16 = jnp.bfloat16
f32 = jnp.float32


def silu(rows):
    x = rows.astype(f32)
    return (x * jax.nn.sigmoid(x)).astype(bf16)


def states_kernel(k_ref, v_ref, s_ref):
    for h in range(s_ref.shape[0]):
        cols = slice(h * DH, (h + 1) * DH)
        ka = silu(k_ref[0, :, cols])
        s_ref[h] = lax.dot_general(
            ka, v_ref[0, :, cols], (((0,), (0,)), ((), ())), preferred_element_type=f32
        ).astype(bf16)


def local_states(k, v, step):
    _, rows, width = k.shape
    heads = width // DH
    spec = pl.BlockSpec((1, rows, step * DH), lambda i: (0, 0, i))
    return pl.pallas_call(
        states_kernel,
        grid=(heads // step,),
        in_specs=[spec, spec],
        out_specs=pl.BlockSpec((step, DH, DH), lambda i: (i, 0, 0)),
        out_shape=jax.ShapeDtypeStruct((heads, DH, DH), bf16),
        name="states",
    )(k, v)


def total_kernel(s_ref, t_ref):
    total = s_ref[0].astype(f32)
    for r in range(1, s_ref.shape[0]):
        total = total + s_ref[r].astype(f32)
    t_ref[...] = total.astype(bf16)


def prefix_kernel(z_ref, s_ref, t_ref, p_ref):
    z = z_ref[0]
    running = jnp.zeros(t_ref.shape[1:], f32)
    for r in range(t_ref.shape[0]):
        running = running + jnp.where(r < z, t_ref[r].astype(f32), 0.0)
    for r in range(s_ref.shape[0]):
        p_ref[r] = running.astype(bf16)
        running = running + s_ref[r].astype(f32)


def output_kernel(q_ref, k_ref, v_ref, p_ref, g_ref, o_ref):
    rows = q_ref.shape[1]
    keep = lax.broadcasted_iota(jnp.int32, (rows, rows), 0) >= lax.broadcasted_iota(
        jnp.int32, (rows, rows), 1
    )
    for h in range(p_ref.shape[0]):
        cols = slice(h * DH, (h + 1) * DH)
        qa = silu(q_ref[0, :, cols])
        ka = silu(k_ref[0, :, cols])
        scores = lax.dot_general(qa, ka, (((1,), (1,)), ((), ())), preferred_element_type=f32)
        scores = jnp.where(keep, scores, 0.0).astype(bf16)
        o = jnp.dot(scores, v_ref[0, :, cols], preferred_element_type=f32)
        o = o + jnp.dot(qa, p_ref[h], preferred_element_type=f32)
        mean = jnp.mean(o * o, axis=-1, keepdims=True)
        normed = (o * lax.rsqrt(mean + EPSILON)).astype(bf16)
        o_ref[0, :, cols] = (normed.astype(f32) * g_ref[:, cols]).astype(bf16)


def outputs(q, k, v, prefix, gain, step):
    _, rows, width = q.shape
    heads = width // DH
    spec = pl.BlockSpec((1, rows, step * DH), lambda i: (0, 0, i))
    return pl.pallas_call(
        output_kernel,
        grid=(heads // step,),
        in_specs=[
            spec,
            spec,
            spec,
            pl.BlockSpec((step, DH, DH), lambda i: (i, 0, 0)),
            pl.BlockSpec((1, step * DH), lambda i: (0, i)),
        ],
        out_specs=spec,
        out_shape=jax.ShapeDtypeStruct(q.shape, bf16),
        name="outputs",
    )(q, k, v, prefix, gain)


def local(queries, key_rows, value_rows, head_gain):
    states = local_states(key_rows, value_rows, 8)
    mine = lax.all_to_all(states, PLANE, 0, 0, tiled=True)
    total = pl.pallas_call(
        total_kernel, out_shape=jax.ShapeDtypeStruct(mine.shape[1:], bf16), name="total"
    )(mine)
    totals = lax.all_gather(total, "z")
    z = lax.axis_index("z").astype(jnp.int32).reshape(1)
    vmem = pl.BlockSpec(memory_space=pltpu.VMEM)
    prefixes = pl.pallas_call(
        prefix_kernel,
        in_specs=[pl.BlockSpec(memory_space=pltpu.SMEM), vmem, vmem],
        out_specs=vmem,
        out_shape=jax.ShapeDtypeStruct(mine.shape, bf16),
        name="prefix",
    )(z, mine, totals)
    prefix = lax.all_to_all(prefixes, PLANE, 0, 0, tiled=True)
    return outputs(queries, key_rows, value_rows, prefix, head_gain[None, :], 8)


def solution(mesh):
    torus = Mesh(mesh.devices.reshape(4, 2, 16, 4), ("y", "core", "z", "x"))
    spec = P(("z", "x"), ("y", "core"), None)
    return jax.shard_map(
        local, mesh=torus, in_specs=(spec, spec, spec, P()), out_specs=spec, check_vma=False
    )
```

time: 181 us -> 103 us (0.57)
  waiting for transfers between devices: 76.7 us -> 17 us
  blocking collectives: 38.2 us -> 60.6 us
  Pallas kernels: 0 us -> 14 us
  between operations: 13.5 us -> 0.02 us
  starting transfers between devices: 22.5 us -> 10.4 us
  local copies, waits for them, and re-layouts: 11.2 us -> 0.97 us
  other arithmetic: 9.42 us -> 0 us
  matrix products: 8.83 us -> 0 us
    all_gather x1 -> x0, waiting for transfers between devices: 34.4 us -> none  [prefix_by_axis(): pieces = lax.all_gather(total.astype(jnp.bfloat16), axis)]
    all_to_all x3 -> x1, waiting for transfers between devices: 42.3 us -> 17 us  [local(): mine = lax.all_to_all(states, PLANE, 0, 0, tiled=True)]
    all_gather x1, blocking collectives: 9.9 us -> 31.6 us  [local(): totals = lax.all_gather(total, 'z')]
    pallas_call x0 -> x4, Pallas kernels: none -> 14 us  [the longest x1 5.32 us: outputs(): pl.pallas_call(output_kernel, grid=(heads // step,), in_specs=[spec, spec...]
    all_to_all x3 -> x1, starting transfers between devices: 22.5 us -> 10.4 us  [local(): mine = lax.all_to_all(states, PLANE, 0, 0, tiled=True)]
    dot_general x3 -> x0, matrix products: 8.83 us -> none  [the longest x1 5.42 us: attend(): jnp.einsum('nhij,njhe->nihe', scores, block_v, preferred_element_type=jnp...]
    convert_element_type x6 -> x0, other arithmetic: 6.8 us -> none  [the longest x2 3.05 us: activate(): return jax.nn.silu(rows.astype(jnp.float32)).astype(jnp.bfloat16)]
    convert_element_type x3 -> x0, local copies, waits for them, and re-layouts: 3.99 us -> none  [the longest x1 1.86 us: local(): flat.astype(jnp.float32) * head_gain[None, :]]
  transfers between devices with their start and end apart: 4 -> 1, of which waited for: 4 -> 1; matrix products, arithmetic and copies ran while one was open for 6% -> 0% of each run, Pallas kernels for 0% -> 0%
where the time goes in v1:
time: 103 us
  blocking collectives  60.6 us (59%)
  waiting for transfers between devices  17 us (17%)
  Pallas kernels  14 us (14%)
  starting transfers between devices  10.4 us (10%)
    all_gather x1, blocking collectives, local(): totals = lax.all_gather(total, 'z')  31.6 us
    all_to_all x1, blocking collectives, local(): prefix = lax.all_to_all(prefixes, PLANE, 0, 0, tiled=True)  29 us
    all_to_all x1, waiting for transfers between devices, local(): mine = lax.all_to_all(states, PLANE, 0, 0, tiled=True)  17 us
    all_to_all x1, starting transfers between devices, local(): mine = lax.all_to_all(states, PLANE, 0, 0, tiled=True)  10.4 us
    pallas_call x1, Pallas kernels, outputs(): pl.pallas_call(output_kernel, grid=(heads // step,), in_specs=[spec, spec...  5.32 us
    pallas_call x1, Pallas kernels, local_states(): pl.pallas_call(states_kernel, grid=(heads // step,), in_specs=[spec, spec...  4.08 us
    pallas_call x1, Pallas kernels, local(): pl.pallas_call(prefix_kernel, in_specs=[pl.BlockSpec(memory_space=pltpu.S...  2.6 us
  transfers between devices with their start and end apart: 1, of which 1 were waited for; matrix products, arithmetic and copies ran while one was open for 0% of the time, Pallas kernels for 0%

profile of v1, /device:TPU:1, one launch (start us, length us, event | category | flops | bytes accessed | tf_op | source)
XLA Modules:
  0.0 103.0 jit_solution(7045747382873995959)
XLA Ops:
  0.0 4.1 %states.1 = bf16[32,128,128]{2,1,0:T(8,128)(2,1)} custom-call(bf16[1,128,4096]{2,1,0:T(8,128)(2,1)} %k_ref.3, bf16[1,128,4096]{2,1,0:T(8,128)(2,1)} %v_ref.3), custom_call_target="tpu_custom_call" | custom-call | tf_op jit(solution)/shard_map/states/pallas_call | solution.py:34
  4.1 10.4 %all-to-all-start = ((bf16[32,128,128]{2,1,0:T(8,128)(2,1)}), bf16[32,128,128]{2,1,0:T(8,128)(2,1)S(1)}, u32[]{:S(2)}, u32[]{:S(2)}) async-start(bf16[32,128,128]{2,1,0:T(8,128)(2,1)} %states.1), calls=%async_computation | async-start | bytes 2097152 | tf_op jit(solution)/shard_map/all_to_all | solution.py:101
  14.5 17.0 %all-to-all-done.s_ref = bf16[32,128,128]{2,1,0:T(8,128)(2,1)S(1)} async-done(((bf16[32,128,128]{2,1,0:T(8,128)(2,1)}), bf16[32,128,128]{2,1,0:T(8,128)(2,1)S(1)}, u32[]{:S(2)}, u32[]{:S(2)}) %all-to-all-start) | async-done | bytes 1048608 | tf_op jit(solution)/shard_map/all_to_all | solution.py:101
  31.5 0.0 copy-start
  31.5 1.0 copy-done
  32.5 2.0 %total.1 = bf16[128,128]{1,0:T(8,128)(2,1)} custom-call(bf16[32,128,128]{2,1,0:T(8,128)(2,1)} %copy-done), custom_call_target="tpu_custom_call" | custom-call | tf_op jit(solution)/shard_map/total/pallas_call | solution.py:102
  34.5 31.6 %all-gather = bf16[2048,128]{1,0:T(8,128)(2,1)} all-gather(bf16[128,128]{1,0:T(8,128)(2,1)} %total.1), channel_id=2, replica_groups=mesh['y'=4,'core'=2,'z'=16,'x'=4] {'z'}, dimensions={0}, use_global_device_ids=true | all-gather | bytes 557056 | tf_op jit(solution)/shard_map/all_gather | solution.py:105
  66.0 2.6 %prefix.1 = bf16[32,128,128]{2,1,0:T(8,128)(2,1)} custom-call(s32[1]{0:T(128)} %bitcast.z_ref, bf16[32,128,128]{2,1,0:T(8,128)(2,1)} %copy-done, bf16[16,128,128]{2,1,0:T(8,128)(2,1)} %bitcast.3), custom_call_target="tpu_custom_call" | custom-call | tf_op jit(solution)/shard_map/prefix/pallas_call | solution.py:108
  68.6 29.0 %all_to_all.10.p_ref = bf16[32,128,128]{2,1,0:T(8,128)(2,1)} all-to-all(bf16[32,128,128]{2,1,0:T(8,128)(2,1)} %prefix.1), channel_id=1, replica_groups=mesh['y'=4,'core'=2,'z'=16,'x'=4] {'x','y','core'}, dimensions={0} | all-to-all | bytes 2097152 | tf_op jit(solution)/shard_map/all_to_all | solution.py:115
  97.6 5.3 %outputs.1 = bf16[1,128,4096]{2,1,0:T(8,128)(2,1)} custom-call(bf16[1,128,4096]{2,1,0:T(8,128)(2,1)} %q_ref.1, bf16[1,128,4096]{2,1,0:T(8,128)(2,1)} %k_ref.3, bf16[1,128,4096]{2,1,0:T(8,128)(2,1)} %v_ref.3, bf16[32,128,128]{2,1,0:T(8,128)(2,1)} %all_to_all.10.p_ref, f32[1,4096]{1,0:T(1,128)} %bitcast.4), custom_call_target="tpu_custom_call" | custom-call | tf_op jit(solution)/shard_map/outputs/pallas_call | solution.py:83
Async XLA Ops:
  4.1 27.4 %all-to-all-start = ((bf16[32,128,128]{2,1,0:T(8,128)(2,1)}), bf16[32,128,128]{2,1,0:T(8,128)(2,1)S(1)}, u32[]{:S(2)}, u32[]{:S(2)}) async-start(bf16[32,128,128]{2,1,0:T(8,128)(2,1)} %states.1), calls=%async_computation | async-start | bytes 2097152 | tf_op jit(solution)/shard_map/all_to_all | solution.py:101
  31.5 1.0 copy-start

commit v2 on v1

v2 whole, which is shorter than its diff:
```python
import jax
import jax.numpy as jnp
from jax import lax
from jax.experimental import pallas as pl
from jax.experimental.pallas import tpu as pltpu
from jax.sharding import Mesh
from jax.sharding import PartitionSpec as P

DH = 128
STEP = 8
CHUNKS = 4
EPSILON = 1e-06
OWNERS = ("z2", "x", "y")
MIB = 2**20
bf16 = jnp.bfloat16
f32 = jnp.float32
VMEM = pl.BlockSpec(memory_space=pltpu.VMEM)
SMEM = pl.BlockSpec(memory_space=pltpu.SMEM)
HBM = pl.BlockSpec(memory_space=pltpu.HBM)


def params(mib):
    return pltpu.CompilerParams(vmem_limit_bytes=mib * MIB)


def stay(array):
    return pltpu.with_memory_space_constraint(array, pltpu.HBM)


def cost(flops):
    return pl.CostEstimate(flops=flops, bytes_accessed=2**21, transcendentals=0)


def silu(rows):
    x = rows.astype(f32)
    return (x * jax.nn.sigmoid(x)).astype(bf16)


def head_cols(h):
    return slice(h * DH, (h + 1) * DH)


def state(k, v):
    contract = (((0,), (0,)), ((), ()))
    return lax.dot_general(silu(k), v, contract, preferred_element_type=f32).astype(bf16)


def given_kernel(k_ref, v_ref, s_ref, k_buf, v_buf, k_sem, v_sem):
    half = 1 - lax.axis_index("core")
    width = k_buf.shape[2]
    heads = width // DH
    copies = []
    for c in range(CHUNKS):
        cols = pl.ds(pl.multiple_of((half * CHUNKS + c) * width, width), width)
        pair = (
            pltpu.make_async_copy(k_ref.at[0, :, cols], k_buf.at[c], k_sem.at[c]),
            pltpu.make_async_copy(v_ref.at[0, :, cols], v_buf.at[c], v_sem.at[c]),
        )
        for copy in pair:
            copy.start()
        copies.append(pair)
    for c in range(CHUNKS):
        for copy in copies[c]:
            copy.wait()
        for h in range(heads):
            s_ref[c * heads + h] = state(k_buf[c, :, head_cols(h)], v_buf[c, :, head_cols(h)])


def given_states(k, v):
    _, rows, width = k.shape
    heads = width // DH // 2
    chunk = (CHUNKS, rows, width // 2 // CHUNKS)
    return pl.pallas_call(
        given_kernel,
        in_specs=[HBM, HBM],
        out_specs=VMEM,
        out_shape=pltpu.VMEM((heads, DH, DH), bf16),
        scratch_shapes=[
            pltpu.VMEM(chunk, bf16),
            pltpu.VMEM(chunk, bf16),
            pltpu.SemaphoreType.DMA((CHUNKS,)),
            pltpu.SemaphoreType.DMA((CHUNKS,)),
        ],
        compiler_params=params(8),
        name="given",
    )(stay(k), stay(v))


def kept_kernel(half_ref, k_ref, v_ref, s_ref):
    for h in range(s_ref.shape[0]):
        s_ref[h] = state(k_ref[0, :, head_cols(h)], v_ref[0, :, head_cols(h)])


def kept_states(k, v, half):
    _, rows, width = k.shape
    heads = width // DH // 2
    spec = pl.BlockSpec((1, rows, width // 2), lambda i, half: (0, 0, half[0]))
    return pl.pallas_call(
        kept_kernel,
        grid_spec=pltpu.PrefetchScalarGridSpec(
            num_scalar_prefetch=1,
            grid=(1,),
            in_specs=[spec, spec],
            out_specs=pl.BlockSpec((heads, DH, DH), lambda i, half: (0, 0, 0)),
        ),
        out_shape=jax.ShapeDtypeStruct((heads, DH, DH), bf16),
        compiler_params=params(8),
        cost_estimate=cost(4 * 10**9),
        name="kept",
    )(half, k, v)


def within_kernel(half_ref, second_ref, q_ref, k_ref, v_ref, e_ref, qa_ref, o_ref):
    rows = q_ref.shape[1]
    keep = lax.broadcasted_iota(jnp.int32, (rows, rows), 0) >= lax.broadcasted_iota(
        jnp.int32, (rows, rows), 1
    )
    second = second_ref[0].astype(f32)
    for h in range(q_ref.shape[2] // DH):
        cols = head_cols(h)
        qa = silu(q_ref[0, :, cols])
        ka = silu(k_ref[0, :, cols])
        scores = lax.dot_general(qa, ka, (((1,), (1,)), ((), ())), preferred_element_type=f32)
        scores = jnp.where(keep, scores, 0.0).astype(bf16)
        qa_ref[0, :, cols] = qa
        here = jnp.dot(scores, v_ref[0, :, cols], preferred_element_type=f32)
        before = jnp.dot(qa, e_ref[h], preferred_element_type=f32)
        o_ref[0, :, cols] = here + second * before


def within(q, k, v, earlier, half, second):
    _, rows, width = q.shape
    blocks = width // DH // 2 // STEP
    tokens = (1, rows, STEP * DH)
    spec = pl.BlockSpec(tokens, lambda i, half, second: (0, 0, half[0] * blocks + i))
    out_spec = pl.BlockSpec(tokens, lambda i, half, second: (0, 0, i))
    shape = (1, rows, width // 2)
    return pl.pallas_call(
        within_kernel,
        grid_spec=pltpu.PrefetchScalarGridSpec(
            num_scalar_prefetch=2,
            grid=(blocks,),
            in_specs=[
                spec,
                spec,
                spec,
                pl.BlockSpec((STEP, DH, DH), lambda i, half, second: (i, 0, 0)),
            ],
            out_specs=[out_spec, out_spec],
        ),
        out_shape=[pltpu.HBM(shape, bf16), pltpu.HBM(shape, f32)],
        compiler_params=params(8),
        cost_estimate=cost(8 * 10**9),
        name="within",
    )(half, second, stay(q), stay(k), stay(v), earlier)


def total_kernel(s_ref, t_ref):
    total = s_ref[0].astype(f32)
    for r in range(1, s_ref.shape[0]):
        total = total + s_ref[r].astype(f32)
    total = total.astype(bf16)
    for r in range(t_ref.shape[0]):
        t_ref[r] = total


def prefix_kernel(z_ref, s_ref, t_ref, p_ref):
    z = z_ref[0]
    running = jnp.zeros(t_ref.shape[1:], f32)
    for r in range(t_ref.shape[0]):
        running = running + jnp.where(r < z, t_ref[r].astype(f32), 0.0)
    for r in range(s_ref.shape[0]):
        p_ref[r] = running.astype(bf16)
        running = running + s_ref[r].astype(f32)


def output_kernel(half_ref, qa_ref, o_ref, p_ref, g_ref, *rest):
    out_ref = rest[-1]
    for h in range(p_ref.shape[0]):
        cols = head_cols(h)
        o = o_ref[0, :, cols] + jnp.dot(qa_ref[0, :, cols], p_ref[h], preferred_element_type=f32)
        mean = jnp.mean(o * o, axis=-1, keepdims=True)
        normed = (o * lax.rsqrt(mean + EPSILON)).astype(bf16)
        out_ref[0, :, cols] = (normed.astype(f32) * g_ref[:, cols]).astype(bf16)


def half_outputs(qa, o, prefix, gain, half, before=None):
    _, rows, width = qa.shape
    tokens = pl.BlockSpec((1, rows, width), lambda i, half: (0, 0, 0))
    in_specs = [
        tokens,
        tokens,
        pl.BlockSpec(prefix.shape, lambda i, half: (0, 0, 0)),
        pl.BlockSpec((1, width), lambda i, half: (0, half[0])),
    ]
    operands = [qa, o, prefix, gain]
    if before is not None:
        in_specs.append(pl.BlockSpec(memory_space=pl.ANY))
        operands.append(before)
    return pl.pallas_call(
        output_kernel,
        grid_spec=pltpu.PrefetchScalarGridSpec(
            num_scalar_prefetch=1,
            grid=(1,),
            in_specs=in_specs,
            out_specs=pl.BlockSpec((1, rows, width), lambda i, half: (0, 0, half[0])),
        ),
        out_shape=jax.ShapeDtypeStruct((1, rows, 2 * width), bf16),
        input_output_aliases={} if before is None else {5: 0},
        compiler_params=params(8),
        cost_estimate=cost(4 * 10**9),
        name="outputs",
    )(half, *operands)


def attend(queries, key_rows, value_rows, head_gain):
    core = lax.axis_index("core").astype(jnp.int32)
    own, other = core.reshape(1), (1 - core).reshape(1)
    z = lax.axis_index("z8").astype(jnp.int32).reshape(1)
    gain = head_gain[None, :]
    own, other, z, gain = lax.optimization_barrier((own, other, z, gain))
    swap = ((0, 1), (1, 0))

    given = given_states(key_rows, value_rows)
    partner = lax.ppermute(given, "core", swap)
    kept = kept_states(key_rows, value_rows, own)
    chip = (kept.astype(f32) + partner.astype(f32)).astype(bf16)
    owners = lax.axis_size(OWNERS)
    pieces = (owners, chip.size // (owners * DH), DH)
    mine = lax.all_to_all(chip.reshape(pieces), OWNERS, 0, 0, tiled=True)
    kept, mine = lax.optimization_barrier((kept, mine))
    gift = lax.ppermute(kept, "core", ((0, 1),))
    planes = lax.axis_size("z8")
    total = pl.pallas_call(
        total_kernel,
        in_specs=[VMEM],
        out_specs=VMEM,
        out_shape=jax.ShapeDtypeStruct((planes,) + mine.shape[1:], bf16),
        compiler_params=params(8),
        name="total",
    )(mine)
    totals = lax.all_to_all(total, "z8", 0, 0, tiled=True)
    qa_own, o_own = within(queries, key_rows, value_rows, partner, own, own)
    qa_other, o_other = within(queries, key_rows, value_rows, gift, other, own)
    prefixes = pl.pallas_call(
        prefix_kernel,
        in_specs=[SMEM, VMEM, VMEM],
        out_specs=VMEM,
        out_shape=jax.ShapeDtypeStruct(mine.shape, bf16),
        compiler_params=params(8),
        name="prefix",
    )(z, mine, totals)
    before = lax.all_to_all(prefixes, OWNERS, 0, 0, tiled=True)
    before = before.reshape(chip.shape)
    arrived = lax.ppermute(before, "core", swap)
    out = half_outputs(qa_own, o_own, before, gain, own)
    return half_outputs(qa_other, o_other, arrived, gain, other, out)


def solution(mesh):
    torus = Mesh(mesh.devices.reshape(4, 2, 8, 2, 4), ("y", "core", "z8", "z2", "x"))
    spec = P(("z8", "z2", "x"), ("y", "core"), None)
    return jax.shard_map(
        attend, mesh=torus, in_specs=(spec, spec, spec, P()), out_specs=spec, check_vma=False
    )
```

time: 103 us -> 81.2 us (0.79)
  blocking collectives: 60.6 us -> 40.3 us
  waiting for transfers between devices: 17 us -> 5.9 us
  starting transfers between devices: 10.4 us -> 21 us
    all_gather x1 -> x0, blocking collectives: 31.6 us -> none  [local(): totals = lax.all_gather(total, 'z')]
    ppermute x0 -> x3, starting transfers between devices: none -> 16.6 us  [the longest x1 8.75 us: attend(): partner = lax.ppermute(given, 'core', swap)]
    all_to_all x1, waiting for transfers between devices: 17 us -> 4.6 us  [attend(): before = lax.all_to_all(prefixes, OWNERS, 0, 0, tiled=True)]
    all_to_all x1 -> x2, blocking collectives: 29 us -> 40.3 us  [the longest x1 27.2 us: attend(): totals = lax.all_to_all(total, 'z8', 0, 0, tiled=True)]
    all_to_all x1, starting transfers between devices: 10.4 us -> 4.33 us  [attend(): before = lax.all_to_all(prefixes, OWNERS, 0, 0, tiled=True)]
    ppermute x0 -> x3, waiting for transfers between devices: none -> 1.31 us  [the longest x1 1.3 us: attend(): partner = lax.ppermute(given, 'core', swap)]
    pallas_call x4 -> x8, Pallas kernels: 14 us -> 13.3 us  [the longest x2 6.29 us: within(): pl.pallas_call(within_kernel, grid_spec=pltpu.PrefetchScalarGridSpec(num_...]
  transfers between devices with their start and end apart: 1 -> 4, of which waited for: 1 -> 2; matrix products, arithmetic and copies ran while one was open for 0% -> 0% of each run, Pallas kernels for 0% -> 10%
where the time goes in v2:
time: 81.2 us; the launch traced here: 80.8 us
  blocking collectives  40.3 us (50%)
  starting transfers between devices  21 us (26%)
  Pallas kernels  13.3 us (16%)
  waiting for transfers between devices  5.9 us (7%)
    all_to_all x1, blocking collectives, attend(): totals = lax.all_to_all(total, 'z8', 0, 0, tiled=True)  27.2 us
    all_to_all x1, blocking collectives, attend(): mine = lax.all_to_all(chip.reshape(pieces), OWNERS, 0, 0, tiled=True)  13.1 us
    ppermute x1, starting transfers between devices, attend(): partner = lax.ppermute(given, 'core', swap)  8.75 us
    ppermute x1, starting transfers between devices, attend(): arrived = lax.ppermute(before, 'core', swap)  6.59 us
    pallas_call x2, Pallas kernels, within(): pl.pallas_call(within_kernel, grid_spec=pltpu.PrefetchScalarGridSpec(num_...  6.29 us
    all_to_all x1, waiting for transfers between devices, attend(): before = lax.all_to_all(prefixes, OWNERS, 0, 0, tiled=True)  4.6 us
    all_to_all x1, starting transfers between devices, attend(): before = lax.all_to_all(prefixes, OWNERS, 0, 0, tiled=True)  4.33 us
    pallas_call x1, Pallas kernels, given_states(): pl.pallas_call(given_kernel, in_specs=[HBM, HBM], out_specs=VMEM, out_sha...  2.89 us
  transfers between devices with their start and end apart: 4, of which 2 were waited for; matrix products, arithmetic and copies ran while one was open for 0% of the time, Pallas kernels for 10%

profile of v2, /device:TPU:1, one launch (start us, length us, event | category | flops | bytes accessed | tf_op | source)
XLA Modules:
  0.0 80.8 jit_solution(15193015549334613159)
XLA Ops:
  0.0 0.0 copy-start
  0.0 0.0 copy-start.1
  0.0 2.9 %given.1 = bf16[16,128,128]{2,1,0:T(8,128)(2,1)} custom-call(bf16[1,128,4096]{2,1,0:T(8,128)(2,1)} %k_ref.7, bf16[1,128,4096]{2,1,0:T(8,128)(2,1)} %v_ref.7), custom_call_target="tpu_custom_call" | custom-call | tf_op jit(solution)/shard_map/given/pallas_call | solution.py:73
  2.9 8.7 %collective-permute-start = (bf16[16,128,128]{2,1,0:T(8,128)(2,1)}, bf16[16,128,128]{2,1,0:T(8,128)(2,1)S(1)}, u32[]{:S(2)}, u32[]{:S(2)}) collective-permute-start(bf16[16,128,128]{2,1,0:T(8,128)(2,1)} %given.1), channel_id=1, source_target_pairs={{0,64},{64,0},{1,65},{65,1},{2,66},{66,2},{3,67},{67,3},{4,68},{68... | collective-permute-start | bytes 1572872 | tf_op jit(solution)/shard_map/ppermute | solution.py:225
  11.7 0.0 copy-done
  11.7 0.0 copy-done.1
  11.7 0.4 kept.1
  12.1 1.3 %collective-permute-done.e_ref = bf16[16,128,128]{2,1,0:T(8,128)(2,1)S(1)} collective-permute-done((bf16[16,128,128]{2,1,0:T(8,128)(2,1)}, bf16[16,128,128]{2,1,0:T(8,128)(2,1)S(1)}, u32[]{:S(2)}, u32[]{:S(2)}) %collective-permute-start) | collective-permute-done | bytes 524320 | tf_op jit(solution)/shard_map/ppermute | solution.py:225
  13.4 0.1 add_convert_fusion
  13.5 13.1 %all_to_all.15.s_ref = bf16[32,64,128]{2,1,0:T(8,128)(2,1)S(1)} all-to-all(bf16[32,64,128]{2,1,0:T(8,128)(2,1)S(1)} %bitcast.10), channel_id=1, replica_groups=mesh['y'=4,'core'=2,'z8'=8,'z2'=2,'x'=4] {'z2','x','y'}, dimensions={0} | all-to-all | bytes 1048576 | tf_op jit(solution)/shard_map/all_to_all | solution.py:230
  26.6 0.1 total.1
  26.7 27.2 %all_to_all.16.t_ref = bf16[8,64,128]{2,1,0:T(8,128)(2,1)S(1)} all-to-all(bf16[8,64,128]{2,1,0:T(8,128)(2,1)S(1)} %total.1), channel_id=1, replica_groups=mesh['y'=4,'core'=2,'z8'=8,'z2'=2,'x'=4] {'z8'}, dimensions={0} | all-to-all | bytes 262144 | tf_op jit(solution)/shard_map/all_to_all | solution.py:242
  54.0 0.9 %prefix.1 = bf16[32,64,128]{2,1,0:T(8,128)(2,1)} custom-call(s32[1]{0:T(128)} %bitcast.2.z_ref, bf16[32,64,128]{2,1,0:T(8,128)(2,1)S(1)} %all_to_all.15.s_ref, bf16[8,64,128]{2,1,0:T(8,128)(2,1)S(1)} %all_to_all.16.t_ref), custom_call_target="tpu_custom_call" | custom-call | tf_op jit(solution)/shard_map/prefix/pallas_call | solution.py:245
  54.9 4.3 %all-to-all-start.2 = ((bf16[32,64,128]{2,1,0:T(8,128)(2,1)}), bf16[32,64,128]{2,1,0:T(8,128)(2,1)S(1)}, u32[]{:S(2)}, u32[]{:S(2)}) async-start(bf16[32,64,128]{2,1,0:T(8,128)(2,1)} %prefix.1), calls=%async_computation.2 | async-start | bytes 1048576 | tf_op jit(solution)/shard_map/all_to_all | solution.py:253
  59.2 1.3 %collective-permute-start.1 = (bf16[16,128,128]{2,1,0:T(8,128)(2,1)S(1)}, bf16[16,128,128]{2,1,0:T(8,128)(2,1)S(1)}, u32[]{:S(2)}, u32[]{:S(2)}) collective-permute-start(bf16[16,128,128]{2,1,0:T(8,128)(2,1)S(1)} %kept.1), channel_id=1, source_target_pairs={{0,64},{1,65},{2,66},{3,67},{4,68},{5,69},{6,70},{7,71},{8,72},{9,... | collective-permute-start | bytes 1572872 | tf_op jit(solution)/shard_map/ppermute | solution.py:232
  60.5 3.1 %within.3 = (bf16[1,128,2048]{2,1,0:T(8,128)(2,1)}, f32[1,128,2048]{2,1,0:T(8,128)}) custom-call(s32[1]{0:T(128)} %bitcast.half_ref.second_ref, s32[1]{0:T(128)} %bitcast.half_ref.second_ref, bf16[1,128,4096]{2,1,0:T(8,128)(2,1)} %q_ref.3, bf16[1,128,4096]{2,1,0:T(8,128)(2,1)} %k_ref.7, bf16[1,128,4096]{2,1,0:T(8,128)(2,1)} %v_ref.7, ...), custom_call_target="tpu_custom_call" | custom-call | flops 8000000000 | bytes 2097152 | tf_op jit(solution)/shard_map/within/pallas_call | solution.py:138
  63.6 4.6 %all-to-all-done.2 = bf16[32,64,128]{2,1,0:T(8,128)(2,1)S(1)} async-done(((bf16[32,64,128]{2,1,0:T(8,128)(2,1)}), bf16[32,64,128]{2,1,0:T(8,128)(2,1)S(1)}, u32[]{:S(2)}, u32[]{:S(2)}) %all-to-all-start.2) | async-done | bytes 524320 | tf_op jit(solution)/shard_map/all_to_all | solution.py:253
  68.2 0.0 copy-start.2
  68.2 0.0 copy-start.4
  68.2 0.0 copy-start.6
  68.2 6.6 %collective-permute-start.2 = (bf16[16,128,128]{2,1,0:T(8,128)(2,1)S(1)}, bf16[16,128,128]{2,1,0:T(8,128)(2,1)S(1)}, u32[]{:S(2)}, u32[]{:S(2)}) collective-permute-start(bf16[16,128,128]{2,1,0:T(8,128)(2,1)S(1)} %bitcast.6), channel_id=1, source_target_pairs={{0,64},{64,0},{1,65},{65,1},{2,66},{66,2},{3,67},{67,3},{4,68},{68... | collective-permute-start | bytes 1572872 | tf_op jit(solution)/shard_map/ppermute | solution.py:255
  74.8 0.0 collective-permute-done.1.e_ref
  74.8 3.1 %within.2 = (bf16[1,128,2048]{2,1,0:T(8,128)(2,1)}, f32[1,128,2048]{2,1,0:T(8,128)}) custom-call(s32[1]{0:T(128)} %bitcast.1.half_ref, s32[1]{0:T(128)} %bitcast.half_ref.second_ref, bf16[1,128,4096]{2,1,0:T(8,128)(2,1)} %q_ref.3, bf16[1,128,4096]{2,1,0:T(8,128)(2,1)} %k_ref.7, bf16[1,128,4096]{2,1,0:T(8,128)(2,1)} %v_ref.7, ...), custom_call_target="tpu_custom_call" | custom-call | flops 8000000000 | bytes 2097152 | tf_op jit(solution)/shard_map/within/pallas_call | solution.py:138
  78.0 0.0 copy-done.2
  78.0 0.0 copy-done.4
  78.0 0.0 copy-done.6
  78.0 0.0 copy-start.3
  78.0 0.0 copy-start.5
  78.0 1.4 %outputs.2.rest_0_ = bf16[1,128,4096]{2,1,0:T(8,128)(2,1)} custom-call(s32[1]{0:T(128)} %bitcast.half_ref.second_ref, bf16[1,128,2048]{2,1,0:T(8,128)(2,1)S(1)} %copy-done.6, f32[1,128,2048]{2,1,0:T(8,128)S(1)} %copy-done.4, bf16[16,128,128]{2,1,0:T(8,128)(2,1)S(1)} %bitcast.7, f32[1,4096]{1,0:T(1,128)S(1)} %bitcast.8), custom_call_target="tpu_custom_call" | custom-call | flops 4000000000 | bytes 2097152 | tf_op jit(solution)/shard_map/outputs/pallas_call | solution.py:200
  79.4 0.0 collective-permute-done.2.p_ref
  79.4 0.0 copy-done.3
  79.4 0.0 copy-done.5
  79.4 1.4 %outputs.3 = bf16[1,128,4096]{2,1,0:T(8,128)(2,1)} custom-call(s32[1]{0:T(128)} %bitcast.1.half_ref, bf16[1,128,2048]{2,1,0:T(8,128)(2,1)S(1)} %copy-done.5, f32[1,128,2048]{2,1,0:T(8,128)S(1)} %copy-done.3, bf16[16,128,128]{2,1,0:T(8,128)(2,1)S(1)} %collective-permute-done.2.p_ref, f32[1,4096]{1,0:T(1,128)S(1)} %bitcast.9, ...), custom_call_target="tpu_custom_call", output_to_operand_aliasing={{}: (5, {})} | custom-call | flops 4000000000 | bytes 2097152 | tf_op jit(solution)/shard_map/outputs/pallas_call | solution.py:200
Async XLA Ops:
  0.0 11.7 %copy-start = (bf16[1,128,4096]{2,1,0:T(8,128)(2,1)S(1)}, bf16[1,128,4096]{2,1,0:T(8,128)(2,1)}, u32[]{:S(2)}) copy-start(bf16[1,128,4096]{2,1,0:T(8,128)(2,1)} %k_ref.7) | copy-start | bytes 3145732
  0.0 11.7 %copy-start.1 = (bf16[1,128,4096]{2,1,0:T(8,128)(2,1)S(1)}, bf16[1,128,4096]{2,1,0:T(8,128)(2,1)}, u32[]{:S(2)}) copy-start(bf16[1,128,4096]{2,1,0:T(8,128)(2,1)} %v_ref.7) | copy-start | bytes 3145732
  2.9 10.5 %collective-permute-start = (bf16[16,128,128]{2,1,0:T(8,128)(2,1)}, bf16[16,128,128]{2,1,0:T(8,128)(2,1)S(1)}, u32[]{:S(2)}, u32[]{:S(2)}) collective-permute-start(bf16[16,128,128]{2,1,0:T(8,128)(2,1)} %given.1), channel_id=1, source_target_pairs={{0,64},{64,0},{1,65},{65,1},{2,66},{66,2},{3,67},{67,3},{4,68},{68... | collective-permute-start | bytes 1572872 | tf_op jit(solution)/shard_map/ppermute | solution.py:225
  54.9 13.4 %all-to-all-start.2 = ((bf16[32,64,128]{2,1,0:T(8,128)(2,1)}), bf16[32,64,128]{2,1,0:T(8,128)(2,1)S(1)}, u32[]{:S(2)}, u32[]{:S(2)}) async-start(bf16[32,64,128]{2,1,0:T(8,128)(2,1)} %prefix.1), calls=%async_computation.2 | async-start | bytes 1048576 | tf_op jit(solution)/shard_map/all_to_all | solution.py:253
  59.2 15.6 %collective-permute-start.1 = (bf16[16,128,128]{2,1,0:T(8,128)(2,1)S(1)}, bf16[16,128,128]{2,1,0:T(8,128)(2,1)S(1)}, u32[]{:S(2)}, u32[]{:S(2)}) collective-permute-start(bf16[16,128,128]{2,1,0:T(8,128)(2,1)S(1)} %kept.1), channel_id=1, source_target_pairs={{0,64},{1,65},{2,66},{3,67},{4,68},{5,69},{6,70},{7,71},{8,72},{9,... | collective-permute-start | bytes 1572872 | tf_op jit(solution)/shard_map/ppermute | solution.py:232
  68.2 9.8 %copy-start.2 = (f32[4096]{0:T(1024)S(1)}, f32[4096]{0:T(1024)}, u32[]{:S(2)}) copy-start(f32[4096]{0:T(1024)} %param.7) | copy-start | bytes 49156
  68.2 9.8 %copy-start.4 = (f32[1,128,2048]{2,1,0:T(8,128)S(1)}, f32[1,128,2048]{2,1,0:T(8,128)}, u32[]{:S(2)}) copy-start(f32[1,128,2048]{2,1,0:T(8,128)} %get-tuple-element.24.o_ref) | copy-start | bytes 3145732
  68.2 9.8 %copy-start.6 = (bf16[1,128,2048]{2,1,0:T(8,128)(2,1)S(1)}, bf16[1,128,2048]{2,1,0:T(8,128)(2,1)}, u32[]{:S(2)}) copy-start(bf16[1,128,2048]{2,1,0:T(8,128)(2,1)} %get-tuple-element.23.qa_ref) | copy-start | bytes 1572868
  68.2 11.2 %collective-permute-start.2 = (bf16[16,128,128]{2,1,0:T(8,128)(2,1)S(1)}, bf16[16,128,128]{2,1,0:T(8,128)(2,1)S(1)}, u32[]{:S(2)}, u32[]{:S(2)}) collective-permute-start(bf16[16,128,128]{2,1,0:T(8,128)(2,1)S(1)} %bitcast.6), channel_id=1, source_target_pairs={{0,64},{64,0},{1,65},{65,1},{2,66},{66,2},{3,67},{67,3},{4,68},{68... | collective-permute-start | bytes 1572872 | tf_op jit(solution)/shard_map/ppermute | solution.py:255
  78.0 1.4 %copy-start.3 = (f32[1,128,2048]{2,1,0:T(8,128)S(1)}, f32[1,128,2048]{2,1,0:T(8,128)}, u32[]{:S(2)}) copy-start(f32[1,128,2048]{2,1,0:T(8,128)} %get-tuple-element.19.o_ref) | copy-start | bytes 3145732
  78.0 1.4 %copy-start.5 = (bf16[1,128,2048]{2,1,0:T(8,128)(2,1)S(1)}, bf16[1,128,2048]{2,1,0:T(8,128)(2,1)}, u32[]{:S(2)}) copy-start(bf16[1,128,2048]{2,1,0:T(8,128)(2,1)} %get-tuple-element.18.qa_ref) | copy-start | bytes 1572868

commit v3 on v1

v3 whole, which is shorter than its diff:
```python
import functools

import jax
import jax.numpy as jnp
from jax import lax
from jax.experimental import pallas as pl
from jax.experimental.pallas import tpu as pltpu
from jax.sharding import Mesh
from jax.sharding import PartitionSpec as P


DH = 128
CHUNKS = 4
PARTS = 4
EARLY = 2
EPSILON = 1e-06
OWNERS = ("z2", "x", "y")
MIB = 2**20
bf16 = jnp.bfloat16
f32 = jnp.float32
VMEM = pl.BlockSpec(memory_space=pltpu.VMEM)
HBM = pl.BlockSpec(memory_space=pltpu.HBM)
DMA = pltpu.SemaphoreType.DMA


def params(mib):
    return pltpu.CompilerParams(vmem_limit_bytes=mib * MIB)


def stay(array):
    return pltpu.with_memory_space_constraint(array, pltpu.HBM)


def cost(flops):
    return pl.CostEstimate(flops=flops, bytes_accessed=2**21, transcendentals=0)


def silu(rows):
    x = rows.astype(f32)
    return (x * jax.nn.sigmoid(x)).astype(bf16)


def head_cols(h, start=0):
    return slice(start + h * DH, start + (h + 1) * DH)


def states_kernel(own, k_ref, v_ref, s_ref, k_buf, v_buf, sems):
    core = lax.axis_index("core")
    half = core if own else 1 - core
    width = k_buf.shape[1]
    cols = pl.ds(pl.multiple_of(half * width, width), width)
    copies = (
        pltpu.make_async_copy(k_ref.at[0, :, cols], k_buf, sems.at[0]),
        pltpu.make_async_copy(v_ref.at[0, :, cols], v_buf, sems.at[1]),
    )
    for copy in copies:
        copy.start()
    for copy in copies:
        copy.wait()
    for h in range(s_ref.shape[0]):
        s_ref[h] = lax.dot_general(
            silu(k_buf[:, head_cols(h)]),
            v_buf[:, head_cols(h)],
            (((0,), (0,)), ((), ())),
            preferred_element_type=f32,
        ).astype(bf16)


def half_states(k, v, own):
    _, rows, width = k.shape
    heads = width // DH // 2
    half = pltpu.VMEM((rows, width // 2), bf16)
    return pl.pallas_call(
        functools.partial(states_kernel, own),
        in_specs=[HBM, HBM],
        out_specs=VMEM,
        out_shape=pltpu.VMEM((heads, DH, DH), bf16),
        scratch_shapes=[half, half, DMA((2,))],
        compiler_params=params(8),
        cost_estimate=cost(4 * 10**9),
    )(stay(k), stay(v))


def within_kernel(low, high, *refs):
    z = lax.axis_index("z8")

    @pl.when(jnp.logical_and(z >= low, z < high))
    def _():
        within_body(*refs[:3], *refs[-9:])


def within_body(q_ref, k_ref, v_ref, own_ref, other_ref, q_buf, k_buf, buf, q_sem, k_sem, v_sem, out_sem):
    core = lax.axis_index("core")
    rows, width = q_buf.shape[1:]
    per_half = CHUNKS // 2
    keep = lax.broadcasted_iota(jnp.int32, (rows, rows), 0) >= lax.broadcasted_iota(
        jnp.int32, (rows, rows), 1
    )
    loads = []
    for c in range(CHUNKS):
        half = core if c < per_half else 1 - core
        block = half * per_half + c % per_half
        cols = pl.ds(pl.multiple_of(block * width, width), width)
        copies = (
            pltpu.make_async_copy(q_ref.at[0, :, cols], q_buf.at[c], q_sem.at[c]),
            pltpu.make_async_copy(k_ref.at[0, :, cols], k_buf.at[c], k_sem.at[c]),
            pltpu.make_async_copy(
                v_ref.at[0, :, cols], buf.at[c, :, pl.ds(2 * width, width)], v_sem.at[c]
            ),
        )
        for copy in copies:
            copy.start()
        loads.append(copies)
    stores = []
    for c in range(CHUNKS):
        for copy in loads[c]:
            copy.wait()
        for h in range(width // DH):
            qa = silu(q_buf[c, :, head_cols(h)])
            ka = silu(k_buf[c, :, head_cols(h)])
            scores = lax.dot_general(qa, ka, (((1,), (1,)), ((), ())), preferred_element_type=f32)
            buf[c, :, head_cols(2 * h)] = jnp.where(keep, scores, 0.0).astype(bf16)
            buf[c, :, head_cols(2 * h + 1)] = qa
        target = own_ref if c < per_half else other_ref
        cols = pl.ds((c % per_half) * 3 * width, 3 * width)
        store = pltpu.make_async_copy(buf.at[c], target.at[0, :, cols], out_sem.at[c])
        store.start()
        stores.append(store)
    for store in stores:
        store.wait()


def within(q, k, v, low, high, before):
    _, rows, width = q.shape
    chunk = width // CHUNKS
    out = pltpu.HBM((1, rows, 3 * width // 2), bf16)
    return pl.pallas_call(
        functools.partial(within_kernel, low, high),
        in_specs=[HBM] * 3 + [pl.BlockSpec(memory_space=pl.ANY)] * len(before),
        out_specs=[HBM, HBM],
        out_shape=[out, out],
        scratch_shapes=[
            pltpu.VMEM((CHUNKS, rows, chunk), bf16),
            pltpu.VMEM((CHUNKS, rows, chunk), bf16),
            pltpu.VMEM((CHUNKS, rows, 3 * chunk), bf16),
            DMA((CHUNKS,)),
            DMA((CHUNKS,)),
            DMA((CHUNKS,)),
            DMA((CHUNKS,)),
        ],
        input_output_aliases={3: 0, 4: 1} if low else {},
        compiler_params=params(12),
        cost_estimate=cost(8 * 10**9),
        name="within",
    )(stay(q), stay(k), stay(v), *before)


def merge_kernel(kept_ref, partner_ref, chip_ref, first_ref):
    early = lax.axis_index("core") == 0
    for h in range(kept_ref.shape[0]):
        kept, partner = kept_ref[h].astype(f32), partner_ref[h].astype(f32)
        chip_ref[h] = (kept + partner).astype(bf16)
        first_ref[h] = jnp.where(early, kept, partner).astype(bf16)


def total_kernel(s_ref, t_ref):
    total = s_ref[0].astype(f32)
    for r in range(1, s_ref.shape[0]):
        total = total + s_ref[r].astype(f32)
    t_ref[...] = total.astype(bf16)


def sum_kernel(*refs):
    total = refs[0][...].astype(f32)
    for t_ref in refs[1:-1]:
        total = total + t_ref[...].astype(f32)
    refs[-1][...] = total.astype(bf16)


def prefix_kernel(s_ref, *refs):
    p_ref = refs[-1]
    running = refs[0][...].astype(f32)
    for t_ref in refs[1:-1]:
        running = running + t_ref[...].astype(f32)
    for r in range(s_ref.shape[0]):
        p_ref[r] = running.astype(bf16)
        running = running + s_ref[r].astype(f32)


def hand_over_kernel(before_ref, first_ref, passed_ref, used_ref):
    early = lax.axis_index("core") == 0
    for h in range(before_ref.shape[0]):
        before, first = before_ref[h].astype(f32), first_ref[h].astype(f32)
        passed_ref[h] = (before + jnp.where(early, first, 0.0)).astype(bf16)
        used_ref[h] = (before + jnp.where(early, 0.0, first)).astype(bf16)


def on_chip(kernel, outs, *operands):
    shapes = [jax.ShapeDtypeStruct(shape, bf16) for shape in outs]
    return pl.pallas_call(
        kernel,
        in_specs=[VMEM] * len(operands),
        out_specs=[VMEM] * len(outs),
        out_shape=shapes,
        compiler_params=params(8),
    )(*operands)


def output_kernel(own, sqv_ref, p_ref, g_ref, *rest):
    out_ref, buf, sems = rest[-3:]
    core = lax.axis_index("core")
    half = core if own else 1 - core
    heads = p_ref.shape[0]
    parts, _, width = buf.shape
    per = 2 * heads // CHUNKS
    stores = []
    for h in range(heads):
        part, j = h // (heads // parts), h % (heads // parts)
        start = h // per * 3 * per * DH
        scores_qa = sqv_ref[0, :, start + 2 * (h % per) * DH : start + 2 * (h % per + 1) * DH]
        v = sqv_ref[0, :, head_cols(h % per, start + 2 * per * DH)]
        o = jnp.dot(
            scores_qa, jnp.concatenate([v, p_ref[h]], axis=0), preferred_element_type=f32
        )
        mean = jnp.mean(o * o, axis=-1, keepdims=True)
        normed = (o * lax.rsqrt(mean + EPSILON)).astype(bf16)
        gain = g_ref[:, pl.ds(pl.multiple_of(half * heads * DH + h * DH, DH), DH)]
        buf[part, :, head_cols(j)] = (normed.astype(f32) * gain).astype(bf16)
        if (h + 1) * DH == (part + 1) * width:
            cols = pl.ds(pl.multiple_of((half * parts + part) * width, width), width)
            store = pltpu.make_async_copy(buf.at[part], out_ref.at[0, :, cols], sems.at[part])
            store.start()
            stores.append(store)
    for store in stores:
        store.wait()


def half_outputs(sqv, prefix, gain, own, before=None):
    _, rows, width = sqv.shape
    width = width // 3
    in_specs, operands = [VMEM, VMEM, VMEM], [sqv, prefix, gain]
    if before is not None:
        in_specs.append(HBM)
        operands.append(before)
    return pl.pallas_call(
        functools.partial(output_kernel, own),
        in_specs=in_specs,
        out_specs=HBM,
        out_shape=jax.ShapeDtypeStruct((1, rows, 2 * width), bf16),
        scratch_shapes=[pltpu.VMEM((PARTS, rows, width // PARTS), bf16), DMA((PARTS,))],
        input_output_aliases={} if before is None else {3: 0},
        compiler_params=params(8),
        cost_estimate=cost(4 * 10**9),
        name="outputs",
    )(*operands)


def attend(queries, key_rows, value_rows, head_gain):
    swap = ((0, 1), (1, 0))
    owners, planes = lax.axis_size(OWNERS), lax.axis_size("z8")

    given = half_states(key_rows, value_rows, False)
    partner = lax.ppermute(given, "core", swap)
    kept = half_states(key_rows, value_rows, True)
    half = kept.shape
    chip, first = on_chip(merge_kernel, [half, half], kept, partner)
    pieces = (owners, chip.size // (owners * DH), DH)
    mine = lax.all_to_all(chip.reshape(pieces), OWNERS, 0, 0, tiled=True)
    (total,) = on_chip(total_kernel, [mine.shape[1:]], mine)
    span = planes // 2
    parts = within(queries, key_rows, value_rows, 0, EARLY, [total])
    total, *parts = lax.optimization_barrier((total, *parts))

    def ahead(k, value, low, high):
        return lax.ppermute(value, "z8", [(i, i + k) for i in range(low, high - k)])

    earlier = [ahead(k, total, 0, span - 1) for k in range(span - 2, 0, -1)]
    parts = within(queries, key_rows, value_rows, EARLY, span, parts)
    (front,) = on_chip(sum_kernel, [total.shape], total, *earlier)
    earlier.append(ahead(1, front, span - 2, span))
    (front,) = on_chip(sum_kernel, [total.shape], total, *earlier)
    earlier += [ahead(k, front, span - 1, planes) for k in range(planes - span, 0, -1)]
    sqv_own, sqv_other = within(queries, key_rows, value_rows, span, planes, parts)
    (prefixes,) = on_chip(prefix_kernel, [mine.shape], mine, *earlier)
    before = lax.all_to_all(prefixes, OWNERS, 0, 0, tiled=True)
    before = before.reshape(half)
    passed, used = on_chip(hand_over_kernel, [half, half], before, first)
    arrived = lax.ppermute(passed, "core", swap)
    gain = head_gain[None, :]
    out = half_outputs(sqv_own, used, gain, True)
    return half_outputs(sqv_other, arrived, gain, False, out)


def solution(mesh):
    torus = Mesh(mesh.devices.reshape(4, 2, 8, 2, 4), ("y", "core", "z8", "z2", "x"))
    spec = P(("z8", "z2", "x"), ("y", "core"), None)
    return jax.shard_map(
        attend, mesh=torus, in_specs=(spec, spec, spec, P()), out_specs=spec, check_vma=False
    )
```

time: 103 us -> 71.8 us (0.70)
  the two profiles are of different devices: /device:TPU:1 before, /device:TPU:417 now
where the time goes in v3:
time: 71.8 us; the launch traced here: 71.3 us
  starting transfers between devices  23.8 us (33%)
  blocking collectives  18.1 us (25%)
  waiting for transfers between devices  16.5 us (23%)
  Pallas kernels  10.8 us (15%)
  local copies, waits for them, and re-layouts  1.73 us (2%)
    all_to_all x1, blocking collectives, attend(): mine = lax.all_to_all(chip.reshape(pieces), OWNERS, 0, 0, tiled=True)  18.1 us
    ppermute x7, starting transfers between devices, ahead(): return lax.ppermute(value, 'z8', [(i, i + k) for i in range(low, high - k)])  8.96 us
    all_to_all x1, waiting for transfers between devices, attend(): before = lax.all_to_all(prefixes, OWNERS, 0, 0, tiled=True)  8.42 us
    ppermute x7, waiting for transfers between devices, ahead(): return lax.ppermute(value, 'z8', [(i, i + k) for i in range(low, high - k)])  8.08 us
    ppermute x1, starting transfers between devices, attend(): arrived = lax.ppermute(passed, 'core', swap)  7.86 us
    all_to_all x1, starting transfers between devices, attend(): before = lax.all_to_all(prefixes, OWNERS, 0, 0, tiled=True)  4.44 us
    pallas_call x3, Pallas kernels, within(): pl.pallas_call(functools.partial(within_kernel, low, high), in_specs=[HBM...  3.71 us
    pallas_call x2, Pallas kernels, half_states(): pl.pallas_call(functools.partial(states_kernel, own), in_specs=[HBM, HBM]...  3.17 us
  transfers between devices with their start and end apart: 10, of which 2 were waited for; matrix products, arithmetic and copies ran while one was open for 0% of the time, Pallas kernels for 9%

profile of v3, /device:TPU:417, one launch (start us, length us, event | category | flops | bytes accessed | tf_op | source)
XLA Modules:
  0.0 71.3 jit_solution(12661584822474607072)
XLA Ops:
  0.0 1.6 %shard_map.47 = bf16[16,128,128]{2,1,0:T(8,128)(2,1)S(1)} custom-call(bf16[1,128,4096]{2,1,0:T(8,128)(2,1)} %refs_1_.5, bf16[1,128,4096]{2,1,0:T(8,128)(2,1)} %refs_2_.5), custom_call_target="tpu_custom_call" | custom-call | flops 4000000000 | bytes 2097152 | tf_op jit(solution)/shard_map/pallas_call | solution.py:73
  1.6 2.6 %collective-permute-start = (bf16[16,128,128]{2,1,0:T(8,128)(2,1)S(1)}, bf16[16,128,128]{2,1,0:T(8,128)(2,1)S(1)}, u32[]{:S(2)}, u32[]{:S(2)}) collective-permute-start(bf16[16,128,128]{2,1,0:T(8,128)(2,1)S(1)} %shard_map.47), channel_id=1, source_target_pairs={{0,64},{64,0},{1,65},{65,1},{2,66},{66,2},{3,67},{67,3},{4,68},{68... | collective-permute-start | bytes 1572872 | tf_op jit(solution)/shard_map/ppermute | solution.py:263
  4.2 1.6 %shard_map.46.kept_ref = bf16[16,128,128]{2,1,0:T(8,128)(2,1)S(1)} custom-call(bf16[1,128,4096]{2,1,0:T(8,128)(2,1)} %refs_1_.5, bf16[1,128,4096]{2,1,0:T(8,128)(2,1)} %refs_2_.5), custom_call_target="tpu_custom_call" | custom-call | flops 4000000000 | bytes 2097152 | tf_op jit(solution)/shard_map/pallas_call | solution.py:73
  5.8 0.0 collective-permute-done.partner_ref
  5.8 0.2 shard_map.48
  6.0 18.1 %all_to_all.10.s_ref = bf16[32,64,128]{2,1,0:T(8,128)(2,1)S(1)} all-to-all(bf16[32,64,128]{2,1,0:T(8,128)(2,1)S(1)} %bitcast.4), channel_id=1, replica_groups=mesh['y'=4,'core'=2,'z8'=8,'z2'=2,'x'=4] {'z2','x','y'}, dimensions={0} | all-to-all | bytes 1048576 | tf_op jit(solution)/shard_map/all_to_all | solution.py:268
  24.1 0.1 shard_map.49.refs_3_.refs_0_
  24.2 0.2 within.3
  24.3 0.7 collective-permute-start.1
  25.0 0.7 collective-permute-start.2
  25.7 0.0 collective-permute-done.1.refs_1_.refs_0_
  25.7 0.0 collective-permute-done.2.refs_2_.refs_1_
  25.7 0.7 collective-permute-start.3
  26.4 0.0 collective-permute-done.3.refs_3_.refs_2_
  26.4 0.7 collective-permute-start.4
  27.1 1.3 %collective-permute-start.5 = (bf16[64,128]{1,0:T(8,128)(2,1)S(1)}, bf16[64,128]{1,0:T(8,128)(2,1)S(1)}, u32[]{:S(2)}, u32[]{:S(2)}) collective-permute-start(bf16[64,128]{1,0:T(8,128)(2,1)S(1)} %shard_map.51), channel_id=1, source_target_pairs={{24,48},{32,56},{25,49},{33,57},{26,50},{34,58},{27,51},{35,59},{2... | collective-permute-start | bytes 49160 | tf_op jit(solution)/shard_map/ppermute | solution.py:275
  28.4 1.3 %collective-permute-start.6 = (bf16[64,128]{1,0:T(8,128)(2,1)S(1)}, bf16[64,128]{1,0:T(8,128)(2,1)S(1)}, u32[]{:S(2)}, u32[]{:S(2)}) collective-permute-start(bf16[64,128]{1,0:T(8,128)(2,1)S(1)} %shard_map.51), channel_id=1, source_target_pairs={{24,40},{32,48},{40,56},{25,41},{33,49},{41,57},{26,42},{34,50},{4... | collective-permute-start | bytes 49160 | tf_op jit(solution)/shard_map/ppermute | solution.py:275
  29.7 3.7 %collective-permute-start.7 = (bf16[64,128]{1,0:T(8,128)(2,1)S(1)}, bf16[64,128]{1,0:T(8,128)(2,1)S(1)}, u32[]{:S(2)}, u32[]{:S(2)}) collective-permute-start(bf16[64,128]{1,0:T(8,128)(2,1)S(1)} %shard_map.51), channel_id=1, source_target_pairs={{24,32},{32,40},{40,48},{48,56},{25,33},{33,41},{41,49},{49,57},{2... | collective-permute-start | bytes 49160 | tf_op jit(solution)/shard_map/ppermute | solution.py:275
  33.4 0.0 collective-permute-done.4.refs_3_
  33.4 8.1 %collective-permute-done.5.refs_4_ = bf16[64,128]{1,0:T(8,128)(2,1)S(1)} collective-permute-done((bf16[64,128]{1,0:T(8,128)(2,1)S(1)}, bf16[64,128]{1,0:T(8,128)(2,1)S(1)}, u32[]{:S(2)}, u32[]{:S(2)}) %collective-permute-start.5) | collective-permute-done | bytes 16416 | tf_op jit(solution)/shard_map/ppermute | solution.py:275
  41.5 0.0 collective-permute-done.6.refs_5_
  41.5 0.0 collective-permute-done.7.refs_6_
  41.5 0.9 %shard_map.52 = bf16[32,64,128]{2,1,0:T(8,128)(2,1)} custom-call(bf16[32,64,128]{2,1,0:T(8,128)(2,1)S(1)} %all_to_all.10.s_ref, bf16[64,128]{1,0:T(8,128)(2,1)S(1)} %collective-permute-done.1.refs_1_.refs_0_, bf16[64,128]{1,0:T(8,128)(2,1)S(1)} %collective-permute-done.2.refs_2_.refs_1_, bf16[64,128]{1,0:T(8,128)(2,1)S(1)} %collective-permute-done.3.refs_3_.refs_2_, ...), custom_call_target="tpu_custom_call" | custom-call | tf_op jit(solution)/shard_map/pallas_call | solution.py:200
  42.4 4.4 %all-to-all-start.1 = ((bf16[32,64,128]{2,1,0:T(8,128)(2,1)}), bf16[32,64,128]{2,1,0:T(8,128)(2,1)S(1)}, u32[]{:S(2)}, u32[]{:S(2)}) async-start(bf16[32,64,128]{2,1,0:T(8,128)(2,1)} %shard_map.52), calls=%async_computation.1 | async-start | bytes 1048576 | tf_op jit(solution)/shard_map/all_to_all | solution.py:285
  46.8 0.2 within.4
  47.0 8.4 %all-to-all-done.1 = bf16[32,64,128]{2,1,0:T(8,128)(2,1)S(1)} async-done(((bf16[32,64,128]{2,1,0:T(8,128)(2,1)}), bf16[32,64,128]{2,1,0:T(8,128)(2,1)S(1)}, u32[]{:S(2)}, u32[]{:S(2)}) %all-to-all-start.1) | async-done | bytes 524320 | tf_op jit(solution)/shard_map/all_to_all | solution.py:285
  55.4 0.3 shard_map.53
  55.7 7.9 %collective-permute-start.8 = (bf16[16,128,128]{2,1,0:T(8,128)(2,1)S(1)}, bf16[16,128,128]{2,1,0:T(8,128)(2,1)S(1)}, u32[]{:S(2)}, u32[]{:S(2)}) collective-permute-start(bf16[16,128,128]{2,1,0:T(8,128)(2,1)S(1)} %get-tuple-element.28), channel_id=1, source_target_pairs={{0,64},{64,0},{1,65},{65,1},{2,66},{66,2},{3,67},{67,3},{4,68},{68... | collective-permute-start | bytes 1572872 | tf_op jit(solution)/shard_map/ppermute | solution.py:288
  63.6 0.0 copy-start
  63.6 3.4 %within.5 = (bf16[1,128,6144]{2,1,0:T(8,128)(2,1)}, bf16[1,128,6144]{2,1,0:T(8,128)(2,1)}) custom-call(bf16[1,128,4096]{2,1,0:T(8,128)(2,1)} %refs_0_.5, bf16[1,128,4096]{2,1,0:T(8,128)(2,1)} %refs_1_.5, bf16[1,128,4096]{2,1,0:T(8,128)(2,1)} %refs_2_.5, ...), custom_call_target="tpu_custom_call", output_to_operand_aliasing={{0}: (3, {}), {1}: (4, {})} | custom-call | flops 8000000000 | bytes 2097152 | tf_op jit(solution)/shard_map/within/pallas_call | solution.py:137
  67.0 0.0 copy-done
  67.0 0.0 copy-start.2
  67.0 1.4 %copy-done.2 = bf16[1,128,6144]{2,1,0:T(8,128)(2,1)S(1)} copy-done((bf16[1,128,6144]{2,1,0:T(8,128)(2,1)S(1)}, bf16[1,128,6144]{2,1,0:T(8,128)(2,1)}, u32[]{:S(2)}) %copy-start.2) | copy-done | bytes 1572888
  68.4 0.0 copy-start.1
  68.4 1.3 %outputs.2.rest_0_ = bf16[1,128,4096]{2,1,0:T(8,128)(2,1)} custom-call(bf16[1,128,6144]{2,1,0:T(8,128)(2,1)S(1)} %copy-done.2, bf16[16,128,128]{2,1,0:T(8,128)(2,1)S(1)} %get-tuple-element.30.p_ref, f32[1,4096]{1,0:T(1,128)S(1)} %bitcast.5), custom_call_target="tpu_custom_call" | custom-call | flops 4000000000 | bytes 2097152 | tf_op jit(solution)/shard_map/outputs/pallas_call | solution.py:245
  69.7 0.0 collective-permute-done.8.p_ref
  69.7 0.3 copy-done.1
  70.0 1.3 %outputs.3 = bf16[1,128,4096]{2,1,0:T(8,128)(2,1)} custom-call(bf16[1,128,6144]{2,1,0:T(8,128)(2,1)S(1)} %copy-done.1, bf16[16,128,128]{2,1,0:T(8,128)(2,1)S(1)} %collective-permute-done.8.p_ref, f32[1,4096]{1,0:T(1,128)S(1)} %bitcast.6, bf16[1,128,4096]{2,1,0:T(8,128)(2,1)} %outputs.2.rest_0_), custom_call_target="tpu_custom_call", output_to_operand_aliasing={{}: (3, {})} | custom-call | flops 4000000000 | bytes 2097152 | tf_op jit(solution)/shard_map/outputs/pallas_call | solution.py:245
  (2 shorter events, 0.0 us)
Async XLA Ops:
  1.6 4.2 %collective-permute-start = (bf16[16,128,128]{2,1,0:T(8,128)(2,1)S(1)}, bf16[16,128,128]{2,1,0:T(8,128)(2,1)S(1)}, u32[]{:S(2)}, u32[]{:S(2)}) collective-permute-start(bf16[16,128,128]{2,1,0:T(8,128)(2,1)S(1)} %shard_map.47), channel_id=1, source_target_pairs={{0,64},{64,0},{1,65},{65,1},{2,66},{66,2},{3,67},{67,3},{4,68},{68... | collective-permute-start | bytes 1572872 | tf_op jit(solution)/shard_map/ppermute | solution.py:263
  24.3 1.3 %collective-permute-start.1 = (bf16[64,128]{1,0:T(8,128)(2,1)S(1)}, bf16[64,128]{1,0:T(8,128)(2,1)S(1)}, u32[]{:S(2)}, u32[]{:S(2)}) collective-permute-start(bf16[64,128]{1,0:T(8,128)(2,1)S(1)} %shard_map.49.refs_3_.refs_0_), channel_id=1, source_target_pairs={{0,16},{1,17},{2,18},{3,19},{4,20},{5,21},{6,22},{7,23},{64,80},{6... | collective-permute-start | bytes 49160 | tf_op jit(solution)/shard_map/ppermute | solution.py:275
  25.0 0.7 collective-permute-start.2
  25.7 0.7 collective-permute-start.3
  26.4 7.0 %collective-permute-start.4 = (bf16[64,128]{1,0:T(8,128)(2,1)S(1)}, bf16[64,128]{1,0:T(8,128)(2,1)S(1)}, u32[]{:S(2)}, u32[]{:S(2)}) collective-permute-start(bf16[64,128]{1,0:T(8,128)(2,1)S(1)} %shard_map.51), channel_id=1, source_target_pairs={{24,56},{25,57},{26,58},{27,59},{28,60},{29,61},{30,62},{31,63},{8... | collective-permute-start | bytes 49160 | tf_op jit(solution)/shard_map/ppermute | solution.py:275
  27.1 14.4 %collective-permute-start.5 = (bf16[64,128]{1,0:T(8,128)(2,1)S(1)}, bf16[64,128]{1,0:T(8,128)(2,1)S(1)}, u32[]{:S(2)}, u32[]{:S(2)}) collective-permute-start(bf16[64,128]{1,0:T(8,128)(2,1)S(1)} %shard_map.51), channel_id=1, source_target_pairs={{24,48},{32,56},{25,49},{33,57},{26,50},{34,58},{27,51},{35,59},{2... | collective-permute-start | bytes 49160 | tf_op jit(solution)/shard_map/ppermute | solution.py:275
  28.4 13.1 %collective-permute-start.6 = (bf16[64,128]{1,0:T(8,128)(2,1)S(1)}, bf16[64,128]{1,0:T(8,128)(2,1)S(1)}, u32[]{:S(2)}, u32[]{:S(2)}) collective-permute-start(bf16[64,128]{1,0:T(8,128)(2,1)S(1)} %shard_map.51), channel_id=1, source_target_pairs={{24,40},{32,48},{40,56},{25,41},{33,49},{41,57},{26,42},{34,50},{4... | collective-permute-start | bytes 49160 | tf_op jit(solution)/shard_map/ppermute | solution.py:275
  29.7 11.8 %collective-permute-start.7 = (bf16[64,128]{1,0:T(8,128)(2,1)S(1)}, bf16[64,128]{1,0:T(8,128)(2,1)S(1)}, u32[]{:S(2)}, u32[]{:S(2)}) collective-permute-start(bf16[64,128]{1,0:T(8,128)(2,1)S(1)} %shard_map.51), channel_id=1, source_target_pairs={{24,32},{32,40},{40,48},{48,56},{25,33},{33,41},{41,49},{49,57},{2... | collective-permute-start | bytes 49160 | tf_op jit(solution)/shard_map/ppermute | solution.py:275
  42.4 13.0 %all-to-all-start.1 = ((bf16[32,64,128]{2,1,0:T(8,128)(2,1)}), bf16[32,64,128]{2,1,0:T(8,128)(2,1)S(1)}, u32[]{:S(2)}, u32[]{:S(2)}) async-start(bf16[32,64,128]{2,1,0:T(8,128)(2,1)} %shard_map.52), calls=%async_computation.1 | async-start | bytes 1048576 | tf_op jit(solution)/shard_map/all_to_all | solution.py:285
  55.7 14.0 %collective-permute-start.8 = (bf16[16,128,128]{2,1,0:T(8,128)(2,1)S(1)}, bf16[16,128,128]{2,1,0:T(8,128)(2,1)S(1)}, u32[]{:S(2)}, u32[]{:S(2)}) collective-permute-start(bf16[16,128,128]{2,1,0:T(8,128)(2,1)S(1)} %get-tuple-element.28), channel_id=1, source_target_pairs={{0,64},{64,0},{1,65},{65,1},{2,66},{66,2},{3,67},{67,3},{4,68},{68... | collective-permute-start | bytes 1572872 | tf_op jit(solution)/shard_map/ppermute | solution.py:288
  63.6 3.4 %copy-start = (f32[4096]{0:T(1024)S(1)}, f32[4096]{0:T(1024)}, u32[]{:S(2)}) copy-start(f32[4096]{0:T(1024)} %param.7) | copy-start | bytes 49156
  67.0 1.4 %copy-start.2 = (bf16[1,128,6144]{2,1,0:T(8,128)(2,1)S(1)}, bf16[1,128,6144]{2,1,0:T(8,128)(2,1)}, u32[]{:S(2)}) copy-start(bf16[1,128,6144]{2,1,0:T(8,128)(2,1)} %get-tuple-element.29.sqv_ref) | copy-start | bytes 4718596
  68.4 1.6 %copy-start.1 = (bf16[1,128,6144]{2,1,0:T(8,128)(2,1)S(1)}, bf16[1,128,6144]{2,1,0:T(8,128)(2,1)}, u32[]{:S(2)}) copy-start(bf16[1,128,6144]{2,1,0:T(8,128)(2,1)} %get-tuple-element.25.sqv_ref) | copy-start | bytes 4718596

commit v4 on v3

--- a/solution.py
+++ b/solution.py
@@ -12,7 +12,7 @@
 DH = 128
 CHUNKS = 4
 PARTS = 4
-EARLY = 2
+EARLY = 1
 EPSILON = 1e-06
 OWNERS = ("z2", "x", "y")
 MIB = 2**20
@@ -274,10 +274,10 @@
     def ahead(k, value, low, high):
         return lax.ppermute(value, "z8", [(i, i + k) for i in range(low, high - k)])
 
-    earlier = [ahead(k, total, 0, span - 1) for k in range(span - 2, 0, -1)]
+    earlier = [ahead(1, total, 0, 2)]
+    (front,) = on_chip(sum_kernel, [total.shape], total, *earlier)
+    earlier += [ahead(k, front, 1, span) for k in range(span - 2, 0, -1)]
     parts = within(queries, key_rows, value_rows, EARLY, span, parts)
-    (front,) = on_chip(sum_kernel, [total.shape], total, *earlier)
-    earlier.append(ahead(1, front, span - 2, span))
     (front,) = on_chip(sum_kernel, [total.shape], total, *earlier)
     earlier += [ahead(k, front, span - 1, planes) for k in range(planes - span, 0, -1)]
     sqv_own, sqv_other = within(queries, key_rows, value_rows, span, planes, parts)

time: 71.8 us -> 69.8 us (0.972)
  waiting for transfers between devices: 16.5 us -> 15.5 us
  starting transfers between devices: 23.8 us -> 23 us
    ppermute x7, waiting for transfers between devices: 8.08 us -> 7.01 us  [ahead(): return lax.ppermute(value, 'z8', [(i, i + k) for i in range(low, high - k)])]
    ppermute x1, starting transfers between devices: 7.86 us -> 6.99 us  [attend(): arrived = lax.ppermute(passed, 'core', swap)]
where the time goes in v4:
time: 69.8 us; the launch traced here: 69.3 us
  starting transfers between devices  23 us (33%)
  blocking collectives  18.1 us (26%)
  waiting for transfers between devices  15.5 us (22%)
  Pallas kernels  10.8 us (15%)
  local copies, waits for them, and re-layouts  1.73 us (2%)
    all_to_all x1, blocking collectives, attend(): mine = lax.all_to_all(chip.reshape(pieces), OWNERS, 0, 0, tiled=True)  18.1 us
    ppermute x7, starting transfers between devices, ahead(): return lax.ppermute(value, 'z8', [(i, i + k) for i in range(low, high - k)])  8.96 us
    all_to_all x1, waiting for transfers between devices, attend(): before = lax.all_to_all(prefixes, OWNERS, 0, 0, tiled=True)  8.45 us
    ppermute x7, waiting for transfers between devices, ahead(): return lax.ppermute(value, 'z8', [(i, i + k) for i in range(low, high - k)])  7.01 us
    ppermute x1, starting transfers between devices, attend(): arrived = lax.ppermute(passed, 'core', swap)  6.99 us
    all_to_all x1, starting transfers between devices, attend(): before = lax.all_to_all(prefixes, OWNERS, 0, 0, tiled=True)  4.42 us
    pallas_call x3, Pallas kernels, within(): pl.pallas_call(functools.partial(within_kernel, low, high), in_specs=[HBM...  3.71 us
    pallas_call x2, Pallas kernels, half_states(): pl.pallas_call(functools.partial(states_kernel, own), in_specs=[HBM, HBM]...  3.17 us
  transfers between devices with their start and end apart: 10, of which 2 were waited for; matrix products, arithmetic and copies ran while one was open for 0% of the time, Pallas kernels for 9%

profile of v4, /device:TPU:417, one launch (start us, length us, event | category | flops | bytes accessed | tf_op | source)
XLA Modules:
  0.0 69.3 jit_solution(13932738052905258114)
XLA Ops:
  0.0 1.6 %shard_map.47 = bf16[16,128,128]{2,1,0:T(8,128)(2,1)S(1)} custom-call(bf16[1,128,4096]{2,1,0:T(8,128)(2,1)} %refs_1_.5, bf16[1,128,4096]{2,1,0:T(8,128)(2,1)} %refs_2_.5), custom_call_target="tpu_custom_call" | custom-call | flops 4000000000 | bytes 2097152 | tf_op jit(solution)/shard_map/pallas_call | solution.py:73
  1.6 2.6 %collective-permute-start = (bf16[16,128,128]{2,1,0:T(8,128)(2,1)S(1)}, bf16[16,128,128]{2,1,0:T(8,128)(2,1)S(1)}, u32[]{:S(2)}, u32[]{:S(2)}) collective-permute-start(bf16[16,128,128]{2,1,0:T(8,128)(2,1)S(1)} %shard_map.47), channel_id=1, source_target_pairs={{0,64},{64,0},{1,65},{65,1},{2,66},{66,2},{3,67},{67,3},{4,68},{68... | collective-permute-start | bytes 1572872 | tf_op jit(solution)/shard_map/ppermute | solution.py:263
  4.2 1.6 %shard_map.46.kept_ref = bf16[16,128,128]{2,1,0:T(8,128)(2,1)S(1)} custom-call(bf16[1,128,4096]{2,1,0:T(8,128)(2,1)} %refs_1_.5, bf16[1,128,4096]{2,1,0:T(8,128)(2,1)} %refs_2_.5), custom_call_target="tpu_custom_call" | custom-call | flops 4000000000 | bytes 2097152 | tf_op jit(solution)/shard_map/pallas_call | solution.py:73
  5.8 0.0 collective-permute-done.partner_ref
  5.8 0.2 shard_map.48
  6.0 18.1 %all_to_all.10.s_ref = bf16[32,64,128]{2,1,0:T(8,128)(2,1)S(1)} all-to-all(bf16[32,64,128]{2,1,0:T(8,128)(2,1)S(1)} %bitcast.4), channel_id=1, replica_groups=mesh['y'=4,'core'=2,'z8'=8,'z2'=2,'x'=4] {'z2','x','y'}, dimensions={0} | all-to-all | bytes 1048576 | tf_op jit(solution)/shard_map/all_to_all | solution.py:268
  24.1 0.1 shard_map.49.refs_3_.refs_0_
  24.2 0.2 within.3
  24.3 0.7 collective-permute-start.1
  25.0 0.0 collective-permute-done.1.refs_1_.refs_0_
  25.0 0.7 collective-permute-start.2
  25.7 0.7 collective-permute-start.3
  26.4 0.0 collective-permute-done.2.refs_2_.refs_1_
  26.4 0.0 collective-permute-done.3.refs_3_.refs_2_
  26.4 0.7 collective-permute-start.4
  27.1 1.3 %collective-permute-start.5 = (bf16[64,128]{1,0:T(8,128)(2,1)S(1)}, bf16[64,128]{1,0:T(8,128)(2,1)S(1)}, u32[]{:S(2)}, u32[]{:S(2)}) collective-permute-start(bf16[64,128]{1,0:T(8,128)(2,1)S(1)} %shard_map.51), channel_id=1, source_target_pairs={{24,48},{32,56},{25,49},{33,57},{26,50},{34,58},{27,51},{35,59},{2... | collective-permute-start | bytes 49160 | tf_op jit(solution)/shard_map/ppermute | solution.py:275
  28.4 1.3 %collective-permute-start.6 = (bf16[64,128]{1,0:T(8,128)(2,1)S(1)}, bf16[64,128]{1,0:T(8,128)(2,1)S(1)}, u32[]{:S(2)}, u32[]{:S(2)}) collective-permute-start(bf16[64,128]{1,0:T(8,128)(2,1)S(1)} %shard_map.51), channel_id=1, source_target_pairs={{24,40},{32,48},{40,56},{25,41},{33,49},{41,57},{26,42},{34,50},{4... | collective-permute-start | bytes 49160 | tf_op jit(solution)/shard_map/ppermute | solution.py:275
  29.7 3.7 %collective-permute-start.7 = (bf16[64,128]{1,0:T(8,128)(2,1)S(1)}, bf16[64,128]{1,0:T(8,128)(2,1)S(1)}, u32[]{:S(2)}, u32[]{:S(2)}) collective-permute-start(bf16[64,128]{1,0:T(8,128)(2,1)S(1)} %shard_map.51), channel_id=1, source_target_pairs={{24,32},{32,40},{40,48},{48,56},{25,33},{33,41},{41,49},{49,57},{2... | collective-permute-start | bytes 49160 | tf_op jit(solution)/shard_map/ppermute | solution.py:275
  33.4 0.0 collective-permute-done.4.refs_3_
  33.4 7.0 %collective-permute-done.5.refs_4_ = bf16[64,128]{1,0:T(8,128)(2,1)S(1)} collective-permute-done((bf16[64,128]{1,0:T(8,128)(2,1)S(1)}, bf16[64,128]{1,0:T(8,128)(2,1)S(1)}, u32[]{:S(2)}, u32[]{:S(2)}) %collective-permute-start.5) | collective-permute-done | bytes 16416 | tf_op jit(solution)/shard_map/ppermute | solution.py:275
  40.4 0.0 collective-permute-done.6.refs_5_
  40.4 0.0 collective-permute-done.7.refs_6_
  40.4 0.9 %shard_map.52 = bf16[32,64,128]{2,1,0:T(8,128)(2,1)} custom-call(bf16[32,64,128]{2,1,0:T(8,128)(2,1)S(1)} %all_to_all.10.s_ref, bf16[64,128]{1,0:T(8,128)(2,1)S(1)} %collective-permute-done.1.refs_1_.refs_0_, bf16[64,128]{1,0:T(8,128)(2,1)S(1)} %collective-permute-done.2.refs_2_.refs_1_, bf16[64,128]{1,0:T(8,128)(2,1)S(1)} %collective-permute-done.3.refs_3_.refs_2_, ...), custom_call_target="tpu_custom_call" | custom-call | tf_op jit(solution)/shard_map/pallas_call | solution.py:200
  41.3 4.4 %all-to-all-start.1 = ((bf16[32,64,128]{2,1,0:T(8,128)(2,1)}), bf16[32,64,128]{2,1,0:T(8,128)(2,1)S(1)}, u32[]{:S(2)}, u32[]{:S(2)}) async-start(bf16[32,64,128]{2,1,0:T(8,128)(2,1)} %shard_map.52), calls=%async_computation.1 | async-start | bytes 1048576 | tf_op jit(solution)/shard_map/all_to_all | solution.py:285
  45.7 0.2 within.4
  45.9 8.5 %all-to-all-done.1 = bf16[32,64,128]{2,1,0:T(8,128)(2,1)S(1)} async-done(((bf16[32,64,128]{2,1,0:T(8,128)(2,1)}), bf16[32,64,128]{2,1,0:T(8,128)(2,1)S(1)}, u32[]{:S(2)}, u32[]{:S(2)}) %all-to-all-start.1) | async-done | bytes 524320 | tf_op jit(solution)/shard_map/all_to_all | solution.py:285
  54.4 0.3 shard_map.53
  54.6 7.0 %collective-permute-start.8 = (bf16[16,128,128]{2,1,0:T(8,128)(2,1)S(1)}, bf16[16,128,128]{2,1,0:T(8,128)(2,1)S(1)}, u32[]{:S(2)}, u32[]{:S(2)}) collective-permute-start(bf16[16,128,128]{2,1,0:T(8,128)(2,1)S(1)} %get-tuple-element.28), channel_id=1, source_target_pairs={{0,64},{64,0},{1,65},{65,1},{2,66},{66,2},{3,67},{67,3},{4,68},{68... | collective-permute-start | bytes 1572872 | tf_op jit(solution)/shard_map/ppermute | solution.py:288
  61.6 0.0 copy-start
  61.6 3.4 %within.5 = (bf16[1,128,6144]{2,1,0:T(8,128)(2,1)}, bf16[1,128,6144]{2,1,0:T(8,128)(2,1)}) custom-call(bf16[1,128,4096]{2,1,0:T(8,128)(2,1)} %refs_0_.5, bf16[1,128,4096]{2,1,0:T(8,128)(2,1)} %refs_1_.5, bf16[1,128,4096]{2,1,0:T(8,128)(2,1)} %refs_2_.5, ...), custom_call_target="tpu_custom_call", output_to_operand_aliasing={{0}: (3, {}), {1}: (4, {})} | custom-call | flops 8000000000 | bytes 2097152 | tf_op jit(solution)/shard_map/within/pallas_call | solution.py:137
  65.0 0.0 copy-done
  65.1 0.0 copy-start.2
  65.1 1.4 %copy-done.2 = bf16[1,128,6144]{2,1,0:T(8,128)(2,1)S(1)} copy-done((bf16[1,128,6144]{2,1,0:T(8,128)(2,1)S(1)}, bf16[1,128,6144]{2,1,0:T(8,128)(2,1)}, u32[]{:S(2)}) %copy-start.2) | copy-done | bytes 1572888
  66.5 0.0 copy-start.1
  66.5 1.3 %outputs.2.rest_0_ = bf16[1,128,4096]{2,1,0:T(8,128)(2,1)} custom-call(bf16[1,128,6144]{2,1,0:T(8,128)(2,1)S(1)} %copy-done.2, bf16[16,128,128]{2,1,0:T(8,128)(2,1)S(1)} %get-tuple-element.30.p_ref, f32[1,4096]{1,0:T(1,128)S(1)} %bitcast.5), custom_call_target="tpu_custom_call" | custom-call | flops 4000000000 | bytes 2097152 | tf_op jit(solution)/shard_map/outputs/pallas_call | solution.py:245
  67.7 0.0 collective-permute-done.8.p_ref
  67.7 0.3 copy-done.1
  68.1 1.3 %outputs.3 = bf16[1,128,4096]{2,1,0:T(8,128)(2,1)} custom-call(bf16[1,128,6144]{2,1,0:T(8,128)(2,1)S(1)} %copy-done.1, bf16[16,128,128]{2,1,0:T(8,128)(2,1)S(1)} %collective-permute-done.8.p_ref, f32[1,4096]{1,0:T(1,128)S(1)} %bitcast.6, bf16[1,128,4096]{2,1,0:T(8,128)(2,1)} %outputs.2.rest_0_), custom_call_target="tpu_custom_call", output_to_operand_aliasing={{}: (3, {})} | custom-call | flops 4000000000 | bytes 2097152 | tf_op jit(solution)/shard_map/outputs/pallas_call | solution.py:245
  (2 shorter events, 0.0 us)
Async XLA Ops:
  1.6 4.2 %collective-permute-start = (bf16[16,128,128]{2,1,0:T(8,128)(2,1)S(1)}, bf16[16,128,128]{2,1,0:T(8,128)(2,1)S(1)}, u32[]{:S(2)}, u32[]{:S(2)}) collective-permute-start(bf16[16,128,128]{2,1,0:T(8,128)(2,1)S(1)} %shard_map.47), channel_id=1, source_target_pairs={{0,64},{64,0},{1,65},{65,1},{2,66},{66,2},{3,67},{67,3},{4,68},{68... | collective-permute-start | bytes 1572872 | tf_op jit(solution)/shard_map/ppermute | solution.py:263
  24.3 0.7 collective-permute-start.1
  25.0 1.3 %collective-permute-start.2 = (bf16[64,128]{1,0:T(8,128)(2,1)S(1)}, bf16[64,128]{1,0:T(8,128)(2,1)S(1)}, u32[]{:S(2)}, u32[]{:S(2)}) collective-permute-start(bf16[64,128]{1,0:T(8,128)(2,1)S(1)} %shard_map.50), channel_id=1, source_target_pairs={{8,24},{9,25},{10,26},{11,27},{12,28},{13,29},{14,30},{15,31},{72,... | collective-permute-start | bytes 49160 | tf_op jit(solution)/shard_map/ppermute | solution.py:275
  25.7 0.7 collective-permute-start.3
  26.4 7.0 %collective-permute-start.4 = (bf16[64,128]{1,0:T(8,128)(2,1)S(1)}, bf16[64,128]{1,0:T(8,128)(2,1)S(1)}, u32[]{:S(2)}, u32[]{:S(2)}) collective-permute-start(bf16[64,128]{1,0:T(8,128)(2,1)S(1)} %shard_map.51), channel_id=1, source_target_pairs={{24,56},{25,57},{26,58},{27,59},{28,60},{29,61},{30,62},{31,63},{8... | collective-permute-start | bytes 49160 | tf_op jit(solution)/shard_map/ppermute | solution.py:275
  27.1 13.3 %collective-permute-start.5 = (bf16[64,128]{1,0:T(8,128)(2,1)S(1)}, bf16[64,128]{1,0:T(8,128)(2,1)S(1)}, u32[]{:S(2)}, u32[]{:S(2)}) collective-permute-start(bf16[64,128]{1,0:T(8,128)(2,1)S(1)} %shard_map.51), channel_id=1, source_target_pairs={{24,48},{32,56},{25,49},{33,57},{26,50},{34,58},{27,51},{35,59},{2... | collective-permute-start | bytes 49160 | tf_op jit(solution)/shard_map/ppermute | solution.py:275
  28.4 12.0 %collective-permute-start.6 = (bf16[64,128]{1,0:T(8,128)(2,1)S(1)}, bf16[64,128]{1,0:T(8,128)(2,1)S(1)}, u32[]{:S(2)}, u32[]{:S(2)}) collective-permute-start(bf16[64,128]{1,0:T(8,128)(2,1)S(1)} %shard_map.51), channel_id=1, source_target_pairs={{24,40},{32,48},{40,56},{25,41},{33,49},{41,57},{26,42},{34,50},{4... | collective-permute-start | bytes 49160 | tf_op jit(solution)/shard_map/ppermute | solution.py:275
  29.7 10.7 %collective-permute-start.7 = (bf16[64,128]{1,0:T(8,128)(2,1)S(1)}, bf16[64,128]{1,0:T(8,128)(2,1)S(1)}, u32[]{:S(2)}, u32[]{:S(2)}) collective-permute-start(bf16[64,128]{1,0:T(8,128)(2,1)S(1)} %shard_map.51), channel_id=1, source_target_pairs={{24,32},{32,40},{40,48},{48,56},{25,33},{33,41},{41,49},{49,57},{2... | collective-permute-start | bytes 49160 | tf_op jit(solution)/shard_map/ppermute | solution.py:275
  41.3 13.0 %all-to-all-start.1 = ((bf16[32,64,128]{2,1,0:T(8,128)(2,1)}), bf16[32,64,128]{2,1,0:T(8,128)(2,1)S(1)}, u32[]{:S(2)}, u32[]{:S(2)}) async-start(bf16[32,64,128]{2,1,0:T(8,128)(2,1)} %shard_map.52), calls=%async_computation.1 | async-start | bytes 1048576 | tf_op jit(solution)/shard_map/all_to_all | solution.py:285
  54.6 13.1 %collective-permute-start.8 = (bf16[16,128,128]{2,1,0:T(8,128)(2,1)S(1)}, bf16[16,128,128]{2,1,0:T(8,128)(2,1)S(1)}, u32[]{:S(2)}, u32[]{:S(2)}) collective-permute-start(bf16[16,128,128]{2,1,0:T(8,128)(2,1)S(1)} %get-tuple-element.28), channel_id=1, source_target_pairs={{0,64},{64,0},{1,65},{65,1},{2,66},{66,2},{3,67},{67,3},{4,68},{68... | collective-permute-start | bytes 1572872 | tf_op jit(solution)/shard_map/ppermute | solution.py:288
  61.6 3.4 %copy-start = (f32[4096]{0:T(1024)S(1)}, f32[4096]{0:T(1024)}, u32[]{:S(2)}) copy-start(f32[4096]{0:T(1024)} %param.7) | copy-start | bytes 49156
  65.1 1.4 %copy-start.2 = (bf16[1,128,6144]{2,1,0:T(8,128)(2,1)S(1)}, bf16[1,128,6144]{2,1,0:T(8,128)(2,1)}, u32[]{:S(2)}) copy-start(bf16[1,128,6144]{2,1,0:T(8,128)(2,1)} %get-tuple-element.29.sqv_ref) | copy-start | bytes 4718596
  66.5 1.6 %copy-start.1 = (bf16[1,128,6144]{2,1,0:T(8,128)(2,1)S(1)}, bf16[1,128,6144]{2,1,0:T(8,128)(2,1)}, u32[]{:S(2)}) copy-start(bf16[1,128,6144]{2,1,0:T(8,128)(2,1)} %get-tuple-element.25.sqv_ref) | copy-start | bytes 4718596
